TPU v7x, 256 devices: a whole 4x4x8 slice. The times are simulated.
256 devices in a mesh: dp: 32 (over z_lo, x, core), cls: 8 (over y, z_hi).
Axes of the slice: x: 4, y: 4, z: 8 (z_hi: 2, z_lo: 4; z = z_hi * 4 + z_lo), core: 2. Of those that a mesh axis runs over, the one named last changes fastest.
Arguments:
- features: bfloat16 [512, 131072], P('cls', 'dp'), may hold values from -200 to 200
- labels: int32 [131072], P('dp'), may hold values from 0 to 7
- coeffs: bfloat16 [8, 512], P('cls'), may hold values from -0.176776695 to 0.176776695
- smoothing: float32 [8], replicated, may hold values from 0.1 to 1
- pair_slots: int32 [40], P('cls'), may hold values from 0 to 39, each once
Outputs:
- hessian: float32 [512, 40, 512], P('dp', 'cls')
- gradient: float32 [8, 512], P('cls', 'dp')
Inputs may be any that keep to these rules, and one draw needn't show every extreme that they name: `pair_slots`: the entry of slot s of the index c of cls is entry c * 5 + s; an entry below 36 names that pair block, a larger entry marks an empty slot; every value appears once.
All inputs are finite; a program needn't handle non-finite values.
Results may differ from a plain program's by a relative error of at most 0.0003.
Values may be sent and summed in bfloat16 or wider, within the bound.
A program may use at most 128 MiB of HBM per device.

v0:
```python
import jax
import jax.numpy as jnp
from jax import lax
from jax.sharding import Mesh
from jax.sharding import PartitionSpec as P

CLASSES = 8
DP = ("dp_0", "dp_1", "dp_2")


def from_everyone(shard, axis):
    count = lax.axis_size(axis)
    return lax.all_to_all(
        jnp.broadcast_to(shard[None], (count, *shard.shape)), axis, 0, 0, tiled=True
    )


def all_in_one(shard, axis):
    leaves = jax.tree.leaves(shard)
    sequence = sorted(range(len(leaves)), key=lambda k: -leaves[k].size)
    width = (1, *leaves[sequence[0]].shape)[-1]
    lines = [
        jnp.pad(leaves[k].reshape(-1), (0, -leaves[k].size % width)).reshape(-1, width)
        for k in sequence
    ]
    both, at, found = (from_everyone(jnp.concatenate(lines), axis), 0, {})
    for k, line in zip(sequence, lines):
        slab = both[:, at : at + len(line)].reshape(len(both), -1)
        found[k] = slab[:, : leaves[k].size].reshape(-1, *leaves[k].shape)
        at += len(line)
    numbers = iter(range(len(leaves)))
    return jax.tree.map(lambda _: found[next(numbers)], shard)


def joined_by_halves(pieces, combine):
    while len(jax.tree.leaves(pieces)[0]) > 1:
        pieces = jax.vmap(combine)(
            *(jax.tree.map(lambda part: part[side::2], pieces) for side in (0, 1))
        )
    return jax.tree.map(lambda part: part[0], pieces)


def joined_all(shard, axis, combine):
    pieces = all_in_one(shard, axis)
    return joined_by_halves(pieces, combine)


def in_order(pieces, dim):
    lengths = list(pieces.shape[1:])
    lengths[dim] *= pieces.shape[0]
    return jnp.moveaxis(pieces, 0, dim).reshape(lengths)


def gathered_copies(shard, axis, dim):
    return in_order(from_everyone(shard, axis), dim)


def cut_along(shard, dim, count):
    before, after = (shard.shape[:dim], shard.shape[dim + 1 :])
    return jnp.moveaxis(shard.reshape(*before, count, -1, *after), dim, 0)


def sum_at_owner(shard, axis, dim):
    pieces = cut_along(shard, dim, lax.axis_size(axis))
    arrived = lax.all_to_all(pieces, axis, split_axis=0, concat_axis=0, tiled=True)
    return arrived.sum(axis=0)


def sum_by_chip(shard, chips, core, dim):
    sizes = (lax.axis_size(chips), lax.axis_size(core))
    pieces = cut_along(shard, dim, sizes[0] * sizes[1])
    inside = pieces.shape[1:]
    pieces = pieces.reshape(*sizes, *inside).swapaxes(0, 1).reshape(-1, *inside)
    pieces = lax.psum_scatter(pieces, core, scatter_dimension=0, tiled=True)
    return lax.psum_scatter(pieces, chips, scatter_dimension=0, tiled=True)[0]


def pair_tables():
    first_list = []
    second_list = []
    for class_one in range(CLASSES):
        for class_two in range(class_one, CLASSES):
            first_list.append(class_one)
            second_list.append(class_two)
    return (jnp.array(first_list, jnp.int32), jnp.array(second_list, jnp.int32))


def second_differences(width):
    index_row = jnp.arange(width - 2)[:, None]
    index_col = jnp.arange(width)[None, :]
    return (
        (index_col == index_row).astype(jnp.float32)
        - 2.0 * (index_col == index_row + 1).astype(jnp.float32)
        + (index_col == index_row + 2).astype(jnp.float32)
    )


def softmax_combine(earlier, later):
    larger = jnp.maximum(earlier[0], later[0])
    summed = earlier[1] * jnp.exp(earlier[0] - larger) + later[1] * jnp.exp(later[0] - larger)
    return (larger, summed)


def local(features, labels, coeffs, smoothing, pair_slots):
    row_count = features.shape[1]
    width = features.shape[0] * lax.axis_size("cls")
    row_share = width // lax.axis_size(DP)
    local_classes = coeffs.shape[0]
    slot_count = pair_slots.shape[0]
    row_weight = 1.0 / row_count
    gathered = lax.all_gather(features, "cls", axis=0, tiled=True)
    scores = jnp.dot(coeffs, gathered, preferred_element_type=jnp.float32)
    own_top = jnp.max(scores, axis=0)
    own_sum = jnp.sum(jnp.exp(scores - own_top[None, :]), axis=0)
    row_top, row_sum = joined_all((own_top, own_sum), "cls", softmax_combine)
    exponent = jnp.exp(scores - row_top[None, :])
    probs = exponent / row_sum[None, :]
    every_prob = gathered_copies(probs, "cls", 0)
    class_start = lax.axis_index("cls") * local_classes
    own_classes = class_start + jnp.arange(local_classes, dtype=jnp.int32)
    one_hot = (labels[None, :] == own_classes[:, None]).astype(jnp.float32)
    resid = (one_hot - probs).astype(jnp.bfloat16)
    grad_term = (
        lax.dot_general(
            resid, gathered, (((1,), (1,)), ((), ())), preferred_element_type=jnp.float32
        )
        * row_weight
    )
    grad_share = sum_at_owner(grad_term, DP, 1)
    row_start = lax.axis_index(DP) * row_share
    differences = second_differences(width)
    own_columns = lax.dynamic_slice_in_dim(differences, row_start, row_share, 1)
    penalty_rows = jnp.dot(
        own_columns.T,
        differences,
        precision=lax.Precision.HIGHEST,
        preferred_element_type=jnp.float32,
    )
    own_smoothing = lax.dynamic_slice_in_dim(smoothing, class_start, local_classes, 0)
    penalty_part = jnp.dot(
        coeffs.astype(jnp.float32),
        penalty_rows.T,
        precision=lax.Precision.HIGHEST,
        preferred_element_type=jnp.float32,
    )
    gradient = grad_share - own_smoothing[:, None] * penalty_part
    first_tab, second_tab = pair_tables()
    pair_count = first_tab.shape[0]
    live_slot = (pair_slots < pair_count).astype(jnp.float32)
    pair_index = jnp.minimum(pair_slots, pair_count - 1)
    pick_pair = pair_index[:, None] == jnp.arange(pair_count, dtype=jnp.int32)[None, :]
    first_class = jnp.sum(jnp.where(pick_pair, first_tab[None, :], 0), axis=1)
    second_class = jnp.sum(jnp.where(pick_pair, second_tab[None, :], 0), axis=1)
    class_range = jnp.arange(CLASSES, dtype=jnp.int32)[None, :]
    select_first = (first_class[:, None] == class_range).astype(jnp.float32)
    select_second = (second_class[:, None] == class_range).astype(jnp.float32)
    prob_first = jnp.dot(
        select_first,
        every_prob,
        precision=lax.Precision.HIGHEST,
        preferred_element_type=jnp.float32,
    )
    prob_second = jnp.dot(
        select_second,
        every_prob,
        precision=lax.Precision.HIGHEST,
        preferred_element_type=jnp.float32,
    )
    same_class = (first_class == second_class).astype(jnp.float32)
    weights = live_slot[:, None] * (prob_first * (same_class[:, None] - prob_second))
    scaled = (gathered[:, None, :] * weights[None, :, :]).astype(jnp.bfloat16)
    scaled = scaled.reshape(
        row_share * lax.axis_size(("dp_0", "dp_1")) * lax.axis_size("dp_2") * slot_count, row_count
    )
    products = lax.dot_general(
        scaled, gathered, (((1,), (1,)), ((), ())), preferred_element_type=jnp.float32
    )
    own_rows = sum_by_chip(
        products.reshape(
            row_share * lax.axis_size(("dp_0", "dp_1")) * lax.axis_size("dp_2"), slot_count * width
        )
        * row_weight,
        ("dp_0", "dp_1"),
        "dp_2",
        0,
    )
    slot_smoothing = jnp.dot(
        select_first, smoothing, precision=lax.Precision.HIGHEST, preferred_element_type=jnp.float32
    )
    penalty = live_slot * same_class * slot_smoothing
    hessian = (
        own_rows.reshape(row_share, slot_count, width)
        + penalty[None, :, None] * penalty_rows[:, None, :]
    )
    return (hessian, gradient)


def solution(mesh):
    finer = Mesh(mesh.devices.reshape(4, 4, 2, mesh.shape["cls"]), ("dp_0", "dp_1", "dp_2", "cls"))
    placed = (P("cls", DP), P(DP), P("cls", None), P(), P("cls"))
    return jax.shard_map(
        local,
        mesh=finer,
        in_specs=placed,
        out_specs=(P(DP, "cls", None), P("cls", DP)),
        check_vma=False,
    )
```

profile of v0, /device:TPU:8, one launch (start us, length us, event | category | flops | bytes accessed | tf_op | source)
XLA Modules:
  0.0 353.2 jit_solution(10550867101574816613)
XLA Ops:
  7.3 0.7 all-gather.2.cloned.1.call-update
  7.9 111.5 %all-gather.2.cloned.1.call-done = bf16[512,4096]{1,0:T(8,128)(2,1)} async-done(((bf16[64,4096]{1,0:T(8,128)(2,1)}), bf16[512,4096]{1,0:T(8,128)(2,1)}) %all-gather.2.cloned.1.call-update) | async-done | bytes 4194320 | tf_op jit(solution)/shard_map/all_gather | solution.py:111
  119.5 2.8 fusion.21
  122.4 0.8 broadcast_in_dim.26
  123.2 5.1 %all-to-all-start = ((f32[8,2,4096]{2,1,0:T(2,128)}), f32[8,2,4096]{2,1,0:T(2,128)S(1)}, u32[]{:S(2)}, u32[]{:S(2)}) async-start(f32[8,2,4096]{2,1,0:T(2,128)} %broadcast_in_dim.26), calls=%async_computation | async-start | bytes 524288 | tf_op jit(solution)/shard_map/all_to_all | solution.py:13
  128.3 10.2 %all-to-all-done = f32[8,2,4096]{2,1,0:T(2,128)S(1)} async-done(((f32[8,2,4096]{2,1,0:T(2,128)}), f32[8,2,4096]{2,1,0:T(2,128)S(1)}, u32[]{:S(2)}, u32[]{:S(2)}) %all-to-all-start) | async-done | bytes 262176 | tf_op jit(solution)/shard_map/all_to_all | solution.py:13
  138.5 0.2 fusion.30
  140.0 0.7 broadcast_in_dim.28
  140.7 4.3 %all-to-all-start.1 = ((f32[8,1,4096]{2,1,0:T(1,128)}), f32[8,1,4096]{2,1,0:T(1,128)S(1)}, u32[]{:S(2)}, u32[]{:S(2)}) async-start(f32[8,1,4096]{2,1,0:T(1,128)} %broadcast_in_dim.28), calls=%async_computation.1 | async-start | bytes 262144 | tf_op jit(solution)/shard_map/all_to_all | solution.py:13
  145.3 6.5 %convert_element_type.44 = f32[512,4096]{1,0:T(8,128)} convert(bf16[512,4096]{1,0:T(8,128)(2,1)} %all-gather.2.cloned.1.call-done) | non-fusion elementwise | flops 2097152 | bytes 12582912 | tf_op jit(solution)/shard_map/convert_element_type | solution.py:171
  151.8 2.3 all-to-all-done.1
  154.1 0.3 fusion.9
  154.3 0.3 fusion.1
  154.6 13.6 %multiply_convert_fusion = bf16[512,5,4096]{2,1,0:T(8,128)(2,1)} fusion(f32[5,4096]{1,0:T(8,128)S(1)} %fusion.1, f32[512,4096]{1,0:T(8,128)} %convert_element_type.44), kind=kLoop, calls=%fused_computation | loop fusion | flops 20971520 | bytes 29442048 | tf_op jit(solution)/shard_map/convert_element_type | solution.py:171
  168.3 32.8 %convert_element_type.48 = bf16[2560,4096]{1,0:T(8,128)(2,1)} reshape(bf16[512,5,4096]{2,1,0:T(8,128)(2,1)} %multiply_convert_fusion) | data formatting | bytes 41943040 | tf_op jit(solution)/shard_map/convert_element_type | solution.py:171
  201.1 18.0 %convolution_multiply_fusion = f32[2560,512]{1,0:T(8,128)} fusion(bf16[2560,4096]{1,0:T(8,128)(2,1)} %convert_element_type.48, bf16[512,4096]{1,0:T(8,128)(2,1)} %all-gather.2.cloned.1.call-done), kind=kOutput, calls=%fused_computation.1 | convolution fusion | flops 10738728960 | bytes 30408704 | tf_op jit(solution)/shard_map/dot_general | solution.py:175
  219.1 7.5 %mul.122 = f32[16,2,16,2560]{3,2,1,0:T(8,128)} reshape(f32[2560,512]{1,0:T(8,128)} %convolution_multiply_fusion) | data formatting | bytes 10485760 | tf_op jit(solution)/shard_map/mul | solution.py:179
  226.6 5.3 %copy.16 = f32[16,2,16,2560]{3,2,0,1:T(8,128)} copy(f32[16,2,16,2560]{3,2,1,0:T(8,128)} %mul.122) | data formatting | bytes 10485760 | tf_op jit(solution)/shard_map/mul | solution.py:179
  231.9 0.2 reduce-scatter.5.cloned.1.call-start
  232.2 18.4 %reduce-scatter.3.cloned.1.call-done = f32[16,16,2560]{2,1,0:T(8,128)} async-done(((f32[32,16,2560]{2,1,0:T(8,128)}), f32[16,16,2560]{2,1,0:T(8,128)}) %reduce-scatter.3.cloned.1.call-update) | async-done | bytes 2621456 | tf_op jit(solution)/shard_map/reduce_scatter | solution.py:74
  250.7 0.3 convert_add_fusion
  251.0 1.0 fusion.6
  251.9 3.4 fusion.15
  255.3 0.7 transpose_reshape.3
  256.0 7.6 %all-to-all-start.2 = ((f32[32,1,16]{2,1,0:T(1,128)}), f32[32,1,16]{2,1,0:T(1,128)S(1)}, u32[]{:S(2)}, u32[]{:S(2)}) async-start(f32[32,1,16]{2,1,0:T(1,128)} %bitcast.10), calls=%async_computation.4 | async-start | bytes 32768 | tf_op jit(solution)/shard_map/all_to_all | solution.py:65
  263.7 0.2 fusion.5
  263.9 0.7 dynamic_slice.7
  264.5 6.8 %all-to-all-done.2 = f32[32,1,16]{2,1,0:T(1,128)S(1)} async-done(((f32[32,1,16]{2,1,0:T(1,128)}), f32[32,1,16]{2,1,0:T(1,128)S(1)}, u32[]{:S(2)}, u32[]{:S(2)}) %all-to-all-start.2) | async-done | bytes 2080 | tf_op jit(solution)/shard_map/all_to_all | solution.py:65
  271.4 1.3 fusion.4
  272.7 72.1 %reduce-scatter.5.cloned.1.call-done = f32[1,16,2560]{2,1,0:T(8,128)} async-done(((f32[16,16,2560]{2,1,0:T(8,128)}), f32[1,16,2560]{2,1,0:T(8,128)}) %reduce-scatter.5.cloned.1.call-update) | async-done | bytes 163856 | tf_op jit(solution)/shard_map/reduce_scatter | solution.py:75
  344.8 1.0 reshape_squeeze.3
  345.9 0.8 copy.18
  (38 shorter events, 1.7 us)
Async XLA Ops:
  7.2 112.3 %copy-start = (bf16[1,512]{1,0:T(2,128)(2,1)S(1)}, bf16[1,512]{1,0:T(2,128)(2,1)}, u32[]{:S(2)}) copy-start(bf16[1,512]{1,0:T(2,128)(2,1)} %param.9) | copy-start | bytes 3076
  7.2 137.9 %copy-start.3 = (s32[36]{0:T(128)S(1)}, s32[36]{0:T(128)}, u32[]{:S(2)}) copy-start(s32[36]{0:T(128)} %constant.49.clone) | copy-start | bytes 436
  7.2 137.9 %copy-start.4 = (s32[36]{0:T(128)S(1)}, s32[36]{0:T(128)}, u32[]{:S(2)}) copy-start(s32[36]{0:T(128)} %constant.50.clone) | copy-start | bytes 436
  7.2 121.1 %copy-start.2 = (s32[5]{0:T(128)S(1)}, s32[5]{0:T(128)}, u32[]{:S(2)}) copy-start(s32[5]{0:T(128)} %param.11) | copy-start | bytes 64
  7.2 112.3 %all-gather.2.cloned.1.call-start = ((), (), s32[]{:S(2)}) async-start(), calls=%async_computation.5 | async-start | bytes 4718592 | tf_op jit(solution)/shard_map/all_gather | solution.py:111
  123.2 15.3 %all-to-all-start = ((f32[8,2,4096]{2,1,0:T(2,128)}), f32[8,2,4096]{2,1,0:T(2,128)S(1)}, u32[]{:S(2)}, u32[]{:S(2)}) async-start(f32[8,2,4096]{2,1,0:T(2,128)} %broadcast_in_dim.26), calls=%async_computation | async-start | bytes 524288 | tf_op jit(solution)/shard_map/all_to_all | solution.py:13
  140.7 13.3 %all-to-all-start.1 = ((f32[8,1,4096]{2,1,0:T(1,128)}), f32[8,1,4096]{2,1,0:T(1,128)S(1)}, u32[]{:S(2)}, u32[]{:S(2)}) async-start(f32[8,1,4096]{2,1,0:T(1,128)} %broadcast_in_dim.28), calls=%async_computation.1 | async-start | bytes 262144 | tf_op jit(solution)/shard_map/all_to_all | solution.py:13
  145.1 105.5 %reduce-scatter.3.cloned.1.call-start = ((), (), s32[]{:S(2)}) async-start(), calls=%async_computation.6 | async-start | bytes 7864320 | tf_op jit(solution)/shard_map/reduce_scatter | solution.py:74
  231.9 18.7 %copy-start.1 = (s32[4096]{0:T(1024)S(1)}, s32[4096]{0:T(1024)}, u32[]{:S(2)}) copy-start(s32[4096]{0:T(1024)} %param.8) | copy-start | bytes 49156
  231.9 31.7 %copy-start.5 = (f32[8]{0:T(128)S(1)}, f32[8]{0:T(128)}, u32[]{:S(2)}) copy-start(f32[8]{0:T(128)} %param.10) | copy-start | bytes 100
  231.9 112.8 %reduce-scatter.5.cloned.1.call-start = ((), (), s32[]{:S(2)}) async-start(), calls=%async_computation.7 | async-start | bytes 2785280 | tf_op jit(solution)/shard_map/reduce_scatter | solution.py:75
  256.0 15.3 %all-to-all-start.2 = ((f32[32,1,16]{2,1,0:T(1,128)}), f32[32,1,16]{2,1,0:T(1,128)S(1)}, u32[]{:S(2)}, u32[]{:S(2)}) async-start(f32[32,1,16]{2,1,0:T(1,128)} %bitcast.10), calls=%async_computation.4 | async-start | bytes 32768 | tf_op jit(solution)/shard_map/all_to_all | solution.py:65
Sparse Core Ops, SparseCore 0:
  10.7 108.7 all-gather.1
  232.0 18.4 reduce-scatter.2
  253.1 91.5 reduce-scatter.4
where the time goes:
time: 355 us; the launch traced here: 353 us
  waiting for transfers between devices  222 us (63%)
  local copies, waits for them, and re-layouts  51.6 us (15%)
  matrix products  27.2 us (8%)
  other arithmetic  21 us (6%)
  starting transfers between devices  17.3 us (5%)
  between operations  14 us (4%)
    all_gather x1, waiting for transfers between devices, local(): gathered = lax.all_gather(features, 'cls', axis=0, tiled=True)  112 us
    reduce_scatter x1, waiting for transfers between devices, sum_by_chip(): return lax.psum_scatter(pieces, chips, scatter_dimension=0, tiled=True)[0]  72.1 us
    convert_element_type x1, local copies, waits for them, and re-layouts, local(): scaled = (gathered[:, None, :] * weights[None, :, :]).astype(jnp.bfloat16)  32.8 us
    convert_element_type x2, other arithmetic, local(): scaled = (gathered[:, None, :] * weights[None, :, :]).astype(jnp.bfloat16)  20.1 us
    reduce_scatter x1, waiting for transfers between devices, sum_by_chip(): pieces = lax.psum_scatter(pieces, core, scatter_dimension=0, tiled=True)  18.4 us
    dot_general x1, matrix products, local(): lax.dot_general(scaled, gathered, (((1,), (1,)), ((), ())), preferred_ele...  18 us
    mul x2, local copies, waits for them, and re-layouts, local(): products.reshape(row_share * lax.axis_size(('dp_0', 'dp_1')) * lax.axis_s...  12.8 us
    all_to_all x2, waiting for transfers between devices, from_everyone(): lax.all_to_all(jnp.broadcast_to(shard[None], (count, *shard.shape)), axis...  12.5 us
  transfers between devices with their start and end apart: 6, of which 6 were waited for; matrix products, arithmetic and copies ran while one was open for 4% of the time, Pallas kernels for 0%

commit v1 on v0

v1 whole, which is shorter than its diff:
```python
import jax
import jax.numpy as jnp
from jax import lax
from jax.experimental import pallas as pl
from jax.experimental.pallas import tpu as pltpu
from jax.sharding import Mesh
from jax.sharding import PartitionSpec as P

CLASSES = 8
PAIRS = CLASSES * (CLASSES + 1) // 2
STARTS = (8, 15, 21, 26, 30, 33, 35)
DIAGONAL = (0, 8, 15, 21, 26, 30, 33, 35)
AXES = ("zl", "x", "core", "y", "zh")
DP = ("zl", "x", "core")
CLS = ("y", "zh")
MESH = pl.DeviceIdType.MESH
STEPS = 8
LEVELS = 32767.0
F32 = jnp.float32
BF16 = jnp.bfloat16


def place():
    return {name: lax.axis_index(name) for name in AXES}


def remote(src, dst, send, recv, device):
    return pltpu.make_async_remote_copy(
        src_ref=src, dst_ref=dst, send_sem=send, recv_sem=recv, device_id=device, device_id_type=MESH
    )


def greet(devices):
    barrier = pltpu.get_barrier_semaphore()
    for device in devices:
        pl.semaphore_signal(barrier, inc=1, device_id=device, device_id_type=MESH)
    return barrier, len(devices)


def pair_weights(slots, probs):
    pair = jnp.minimum(slots, PAIRS - 1)
    first = jnp.zeros_like(pair)
    start = jnp.zeros_like(pair)
    for before, at in zip((0,) + STARTS, STARTS):
        later = pair >= at
        first += jnp.where(later, 1, 0)
        start += jnp.where(later, at - before, 0)
    second = pair - start + first
    live = (slots < PAIRS)[:, :1]
    first, second = first[:, :1], second[:, :1]
    prob_first = jnp.zeros_like(probs)
    prob_second = jnp.zeros_like(probs)
    for k in range(CLASSES):
        row = probs[k : k + 1, :]
        prob_first += jnp.where(first == k, row, 0.0)
        prob_second += jnp.where(second == k, row, 0.0)
    same = jnp.where(first == second, 1.0, 0.0)
    return jnp.where(live, prob_first * (same - prob_second), 0.0)


def gather_kernel(
    feat, coeffs, labels, slots,
    part_out, scale_out, grad_out,
    held, total, labs, pairs, tiles, matrix, gsum, lhs,
    own_sem, z_send, z_recv, yo_send, yo_recv, yz_send, yz_recv, op_send, op_recv,
    d_send, d_recv, t_send, t_recv, p_sem, l_sem,
):
    at = place()
    k, y, h = at["core"], at["y"], at["zh"]
    cls = y * 2 + h
    width = held.shape[2]
    half = width // 2
    rows = feat.shape[0]
    kept = feat.shape[1] // 2
    up, down, across = lax.rem(y + 1, 4), lax.rem(y + 3, 4), lax.rem(y + 2, 4)
    antipode, partner = {"zh": 1 - h}, {"core": 1 - k}

    def other(j):
        c = lax.rem(cls + j, 8)
        return c, {"y": c // 2, "zh": lax.rem(c, 2)}

    barrier, count = greet([other(j)[1] for j in range(1, 8)] + [partner])

    lanes = pl.ds(pl.multiple_of(k * half, half), half)

    def band(q, first, size):
        return held.at[q, pl.ds(pl.multiple_of(first, 64), size), lanes]

    def columns(side, q):
        return feat.at[:, pl.ds(pl.multiple_of(side * kept + q * half, half), half)]

    def own_copy(q):
        return pltpu.make_async_copy(columns(h, q), band(q, cls * rows, rows), own_sem.at[q])

    for q in range(STEPS):
        own_copy(q).start()
    label_rows = kept // 128
    own_labels = labels.at[pl.ds(pl.multiple_of(h * label_rows, 8), label_rows)]
    label_copy = pltpu.make_async_copy(own_labels, labs.at[k], l_sem.at[0])
    label_copy.start()

    row8 = lax.broadcasted_iota(jnp.int32, (8, 128), 0)
    mine = jnp.full((8, 128), 40, jnp.int32)
    for s in range(5):
        mine = jnp.where(row8 == s, slots[s], mine)
    pairs[h] = mine
    coeff_rows = coeffs[...].astype(F32)
    pieces = [coeff_rows[:, 128 * j : 128 * (j + 1)] for j in range(4)]
    tiles[cls] = jnp.concatenate(pieces + [jnp.zeros((4, 128), F32)], axis=0)

    total[...] = jnp.zeros_like(total)
    gsum[...] = jnp.zeros_like(gsum)

    pl.semaphore_wait(barrier, count)

    def z_copy(q, c):
        return remote(columns(1 - h, q), band(q, c * rows, rows), z_send.at[q], z_recv.at[q], antipode)

    def yo_copy(q, d, c):
        to = {"y": (up, down)[d]}
        return remote(columns(h, q), band(q, c * rows, rows), yo_send.at[d, q], yo_recv.at[d, q], to)

    def yz_copy(q, d, c):
        to = {"y": (up, down)[d]}
        block = band(q, c * rows, rows)
        return remote(block, block, yz_send.at[d, q], yz_recv.at[d, q], to)

    def op_copy(q, source):
        to = {"y": jnp.where(lax.rem(q, 2) == 0, up, down)}
        block = band(q, source * 2 * rows, 2 * rows)
        return remote(block, block, op_send.at[q], op_recv.at[q], to)

    def d_copy(q, i, source, lane_core):
        wide = pl.ds(pl.multiple_of(lane_core * half, half), half)
        block = held.at[q, pl.ds(pl.multiple_of(source * 2 * rows, 2 * rows), 2 * rows), wide]
        return remote(block, block, d_send.at[i, q], d_recv.at[i, q], partner)

    def tile_copy(j, c):
        _, to = other(j)
        return remote(tiles.at[c], tiles.at[c], t_send.at[j], t_recv.at[8 - j], to)

    def pair_copy(side):
        return remote(pairs.at[side], pairs.at[side], p_sem.at[0], p_sem.at[1], antipode)

    def label_send(core):
        return remote(labs.at[core], labs.at[core], l_sem.at[1], l_sem.at[2], partner)

    for j in range(1, 8):
        tile_copy(j, cls).start()
    pair_copy(h).start()
    for q in range(STEPS):
        z_copy(q, cls).start()
        for d in range(2):
            yo_copy(q, d, cls).start()
    label_copy.wait()
    label_send(k).start()

    for j in range(1, 8):
        c, _ = other(8 - j)
        tile_copy(8 - j, c).wait_recv()
    pair_copy(1 - h).wait_recv()
    label_send(1 - k).wait_recv()
    for c in range(CLASSES):
        tile = tiles[c]
        matrix[c : c + 1, :] = jnp.concatenate([tile[j : j + 1, :] for j in range(4)], axis=1)

    def stage_a(q):
        own_copy(q).wait()
        z_copy(q, y * 2 + 1 - h).wait_recv()
        for d in range(2):
            yz_copy(q, d, y * 2 + 1 - h).start()
        d_copy(q, 0, y, k).start()

    def stage_b(q):
        for d, source in ((0, down), (1, up)):
            yo_copy(q, d, source * 2 + h).wait_recv()
            yz_copy(q, d, source * 2 + 1 - h).wait_recv()
        op_copy(q, jnp.where(lax.rem(q, 2) == 0, down, up)).start()
        d_copy(q, 1, down, k).start()
        d_copy(q, 2, up, k).start()

    def stage_c(q):
        op_copy(q, across).wait_recv()
        d_copy(q, 3, across, k).start()

    def stage_d(q):
        for i, source in enumerate((y, down, up, across)):
            d_copy(q, i, source, 1 - k).wait_recv()
        block = held[q]
        scores = jnp.dot(matrix[...].astype(BF16), block, preferred_element_type=F32)
        exponent = jnp.exp(scores - jnp.max(scores, axis=0, keepdims=True))
        probs = exponent / jnp.sum(exponent, axis=0, keepdims=True)
        weights = pair_weights(pairs[k], probs)
        lab_rows = [labs[core, pl.ds(q * (half // 128) + i, 1), :] for core in range(2) for i in range(half // 128)]
        lab = jnp.concatenate(lab_rows, axis=1)
        one_hot = lax.broadcasted_iota(jnp.int32, (8, width), 0) == lab
        resid = (jnp.where(one_hot, 1.0, 0.0) - probs).astype(BF16)
        contract = (((1,), (1,)), ((), ()))
        gsum[...] += lax.dot_general(resid, block, contract, preferred_element_type=F32)
        wide = block.astype(F32)
        for s in range(5):
            lhs[s % 2] = (wide * weights[s : s + 1, :]).astype(BF16)
            total[s] += lax.dot_general(lhs[s % 2], block, contract, preferred_element_type=F32)

    def step(t, carry):
        @pl.when(t < STEPS)
        def _():
            stage_a(t)

        @pl.when((t >= 1) & (t < STEPS + 1))
        def _():
            stage_b(t - 1)

        @pl.when((t >= 2) & (t < STEPS + 2))
        def _():
            stage_c(t - 2)

        @pl.when(t >= 3)
        def _():
            stage_d(t - 3)

        return carry

    lax.fori_loop(0, STEPS + 3, step, 0)

    scales = jnp.zeros((8, 128), F32)
    for s in range(5):
        block = total[s]
        largest = jnp.max(jnp.max(jnp.abs(block), axis=0, keepdims=True), axis=1, keepdims=True)
        largest = jnp.maximum(largest, 1e-30)
        scales = jnp.where(row8 == s, largest * (1.0 / LEVELS), scales)
        coded = jnp.round(block * (LEVELS / largest)).astype(jnp.int32).astype(jnp.int16)
        for i in range(4):
            for x in range(4):
                first = i * 128 + x * 32
                part_out[x, s, 32 * i : 32 * (i + 1), :] = coded[first : first + 32, :]
    scale_out[...] = scales
    grad_out[...] = gsum[...]

    for j in range(1, 8):
        tile_copy(j, cls).wait_send()
    pair_copy(h).wait_send()
    label_send(k).wait_send()

    def drain(q, carry):
        z_copy(q, cls).wait_send()
        for d in range(2):
            yo_copy(q, d, cls).wait_send()
            yz_copy(q, d, y * 2 + 1 - h).wait_send()
        op_copy(q, across).wait_send()
        for i, source in enumerate((y, down, up, across)):
            d_copy(q, i, source, k).wait_send()
        return carry

    lax.fori_loop(0, STEPS, drain, 0)


def reduce_kernel(
    part, scales, grad, coeffs, slots, smoothing,
    hess_out, grad_out,
    got, got_scale, got_grad, sums, coded, small, far, far_small, pen_row, stage,
    x_send, x_recv, xs_send, xs_recv, xg_send, xg_recv, z_send, z_recv, zs_send, zs_recv, c_sem,
):
    at = place()
    k, x, y, h, zl = at["core"], at["x"], at["y"], at["zh"], at["zl"]
    z = h * 4 + zl

    def near(j):
        return {"x": lax.rem(x + j, 4)}

    def owner(i, e):
        return {"zl": lax.rem(zl + i, 4), "zh": k, "core": lax.rem(k + e, 2)}

    others = [near(j) for j in range(1, 4)]
    for a in range(2):
        for i in range(4):
            for e in range(2):
                if a or i or e:
                    others.append({"zl": lax.rem(zl + i, 4), "zh": lax.rem(h + a, 2), "core": lax.rem(k + e, 2)})
    barrier, count = greet(others)

    row0 = zl * 128 + x * 32 + k * 16
    ia = lax.broadcasted_iota(jnp.int32, (16, 512), 0) + row0
    ib = lax.broadcasted_iota(jnp.int32, (16, 512), 1)
    pen = jnp.zeros((16, 512), F32)
    taps = (1.0, -2.0, 1.0)
    for m in range(3):
        inside = (ia - m >= 0) & (ia - m <= 509)
        for n in range(3):
            pen += jnp.where(inside & (ib - n == ia - m), taps[m] * taps[n], 0.0)
    lane = lax.broadcasted_iota(jnp.int32, (8, 512), 1)
    row = jnp.broadcast_to(coeffs[...].astype(F32), (8, 512))
    diff = row - 2.0 * pltpu.roll(row, 511, 1) + pltpu.roll(row, 510, 1)
    diff = jnp.where(lane < 510, diff, 0.0)
    pen_row[...] = diff - 2.0 * pltpu.roll(diff, 1, 1) + pltpu.roll(diff, 2, 1)

    pl.semaphore_wait(barrier, count)

    def x_copy(s, j, source):
        to = lax.rem(x + j, 4)
        return remote(part.at[to, s], got.at[source, s], x_send.at[j, s], x_recv.at[4 - j, s], near(j))

    def xs_copy(j, source):
        return remote(scales, got_scale.at[source], xs_send.at[j], xs_recv.at[4 - j], near(j))

    def xg_copy(j, source):
        return remote(grad, got_grad.at[source], xg_send.at[j], xg_recv.at[4 - j], near(j))

    for j in (1, 3, 2):
        xs_copy(j, x).start()
    for s in range(5):
        for j in (1, 3, 2):
            x_copy(s, j, x).start()
    for j in (1, 3, 2):
        xg_copy(j, x).start()
    own_scale = pltpu.make_async_copy(scales, got_scale.at[x], c_sem.at[0])
    own_grad = pltpu.make_async_copy(grad, got_grad.at[x], c_sem.at[1])
    own_scale.start()
    own_grad.start()

    def own_part(s):
        return pltpu.make_async_copy(part.at[x, s], got.at[x, s], c_sem.at[2 + s])

    for s in range(5):
        own_part(s).start()
    own_scale.wait()
    own_grad.wait()
    for j in (1, 3, 2):
        xs_copy(4 - j, lax.rem(x + 4 - j, 4)).wait_recv()

    def z_copy(s, i, e, source):
        to = lax.rem(zl + i, 4)
        src = coded.at[s, to, lax.rem(k + e, 2)]
        return remote(src, far.at[source, s], z_send.at[i, e, s], z_recv.at[source, s], owner(i, e))

    def zs_copy(i, e, source):
        to = lax.rem(zl + i, 4)
        return remote(small.at[to], far_small.at[source], zs_send.at[i, e], zs_recv.at[source], owner(i, e))

    def to_owners(act):
        for i in (2, 1, 3, 0):
            for e in range(2):
                if i or e:
                    act(i, e)
                else:
                    pl.when(h != k)(lambda: act(0, 0))

    def own_far(s):
        return pltpu.make_async_copy(coded.at[s, zl, k], far.at[z, s], c_sem.at[8 + s])

    own_small = pltpu.make_async_copy(small.at[zl], far_small.at[z], c_sem.at[7])

    row8 = lax.broadcasted_iota(jnp.int32, (8, 128), 0)
    scale2 = jnp.zeros((8, 128), F32)
    for s in range(5):
        own_part(s).wait()
        for j in (1, 3, 2):
            x_copy(s, 4 - j, lax.rem(x + 4 - j, 4)).wait_recv()
        value = jnp.zeros((128, 512), F32)
        for source in range(4):
            scale = got_scale[source, s : s + 1, 0:1]
            value += got[source, s].astype(jnp.int32).astype(F32) * scale
        largest = jnp.max(jnp.max(jnp.abs(value), axis=0, keepdims=True), axis=1, keepdims=True)
        largest = jnp.maximum(largest, 1e-30)
        scale2 = jnp.where(row8 == s, largest * (1.0 / LEVELS), scale2)
        out = jnp.round(value * (LEVELS / largest)).astype(jnp.int32).astype(jnp.int16)
        for i in range(4):
            for e in range(2):
                first = i * 32 + e * 16
                coded[s, i, e] = out[first : first + 16, :]
        to_owners(lambda i, e: z_copy(s, i, e, z).start())
        pl.when(h == k)(lambda: own_far(s).start())

    for j in (1, 3, 2):
        xg_copy(4 - j, lax.rem(x + 4 - j, 4)).wait_recv()
    all_grad = got_grad[0] + got_grad[1] + got_grad[2] + got_grad[3]
    for i in range(4):
        small[i, 0] = all_grad[:, 128 * i : 128 * (i + 1)]
        small[i, 1] = scale2
    to_owners(lambda i, e: zs_copy(i, e, z).start())
    pl.when(h == k)(lambda: own_small.start())

    def arrived(source, wait):
        def other():
            wait(source)

        pl.when((z != source) | (h != k))(other)

    for source in range(8):
        arrived(source, lambda source: zs_copy(1, 0, source).wait_recv())
    pl.when(h == k)(lambda: own_small.wait())
    grads = far_small[0, 0]
    for source in range(1, 8):
        grads += far_small[source, 0]
    for s in range(5):
        for source in range(8):
            arrived(source, lambda source: z_copy(s, 1, 0, source).wait_recv())
        pl.when(h == k)(lambda: own_far(s).wait())
        value = jnp.zeros((16, 512), F32)
        for source in range(8):
            scale = far_small[source, 1, s : s + 1, 0:1]
            value += far[source, s].astype(jnp.int32).astype(F32) * scale
        smooth = jnp.float32(0.0)
        for j, number in enumerate(DIAGONAL):
            smooth += jnp.where(slots[s] == number, smoothing[j], 0.0)
        hess_out[s] = value * (1.0 / 4096.0) + pen * smooth

    cls = y * 2 + h
    picked = jnp.sum(jnp.where(row8 == cls, grads, 0.0), axis=0, keepdims=True) * (1.0 / 4096.0)
    pen_part = pen_row[:, pl.ds(pl.multiple_of(zl * 128, 128), 128)]
    final = picked - smoothing[cls] * pen_part
    stage[...] = pltpu.roll(final, lax.rem(128 - (x * 32 + k * 16), 128), 1)
    grad_out[...] = stage[0:1, 0:16]

    for j in (1, 3, 2):
        xs_copy(j, x).wait_send()
        xg_copy(j, x).wait_send()
        for s in range(5):
            x_copy(s, j, x).wait_send()
    to_owners(lambda i, e: zs_copy(i, e, z).wait_send())
    for s in range(5):
        to_owners(lambda i, e: z_copy(s, i, e, z).wait_send())


def local(features, labels, coeffs, smoothing, pair_slots):
    vmem = pl.BlockSpec(memory_space=pltpu.VMEM)
    smem = pl.BlockSpec(memory_space=pltpu.SMEM)
    anyspace = pl.BlockSpec(memory_space=pl.ANY)
    dma = pltpu.SemaphoreType.DMA
    half = features.shape[1] // 2 // STEPS
    part, scales, grad = pl.pallas_call(
        gather_kernel,
        out_shape=(
            jax.ShapeDtypeStruct((4, 5, 128, 512), jnp.int16),
            jax.ShapeDtypeStruct((8, 128), F32),
            jax.ShapeDtypeStruct((8, 512), F32),
        ),
        in_specs=[anyspace, vmem, anyspace, smem],
        out_specs=(vmem, vmem, vmem),
        scratch_shapes=[
            pltpu.VMEM((STEPS, 512, 2 * half), BF16),
            pltpu.VMEM((5, 512, 512), F32),
            pltpu.VMEM((2, 16, 128), jnp.int32),
            pltpu.VMEM((2, 8, 128), jnp.int32),
            pltpu.VMEM((8, 8, 128), F32),
            pltpu.VMEM((8, 512), F32),
            pltpu.VMEM((8, 512), F32),
            pltpu.VMEM((2, 512, 2 * half), BF16),
            dma((STEPS,)), dma((STEPS,)), dma((STEPS,)),
            dma((2, STEPS)), dma((2, STEPS)), dma((2, STEPS)), dma((2, STEPS)),
            dma((STEPS,)), dma((STEPS,)),
            dma((4, STEPS)), dma((4, STEPS)),
            dma((8,)), dma((8,)), dma((2,)), dma((3,)),
        ],
        compiler_params=pltpu.CompilerParams(collective_id=0, has_side_effects=True),
        name="gather",
    )(features, coeffs, labels.reshape(32, 128), pair_slots)
    hessian, gradient = pl.pallas_call(
        reduce_kernel,
        out_shape=(
            jax.ShapeDtypeStruct((5, 16, 512), F32),
            jax.ShapeDtypeStruct((1, 16), F32),
        ),
        in_specs=[anyspace, anyspace, anyspace, vmem, smem, smem],
        out_specs=(vmem, vmem),
        scratch_shapes=[
            pltpu.VMEM((4, 5, 128, 512), jnp.int16),
            pltpu.VMEM((4, 8, 128), F32),
            pltpu.VMEM((4, 8, 512), F32),
            pltpu.VMEM((8, 128), F32),
            pltpu.VMEM((5, 4, 2, 16, 512), jnp.int16),
            pltpu.VMEM((4, 2, 8, 128), F32),
            pltpu.VMEM((8, 5, 16, 512), jnp.int16),
            pltpu.VMEM((8, 2, 8, 128), F32),
            pltpu.VMEM((8, 512), F32),
            pltpu.VMEM((8, 128), F32),
            dma((4, 5)), dma((4, 5)), dma((4,)), dma((4,)), dma((4,)), dma((4,)),
            dma((4, 2, 5)), dma((8, 5)), dma((4, 2)), dma((8,)), dma((13,)),
        ],
        compiler_params=pltpu.CompilerParams(collective_id=1, has_side_effects=True),
        name="reduce",
    )(part, scales, grad, coeffs, pair_slots, smoothing)
    return hessian.transpose(1, 0, 2), gradient


def solution(mesh):
    finer = Mesh(mesh.devices.reshape(4, 4, 2, 4, 2), AXES)
    placed = (P(CLS, DP), P(DP), P(CLS, None), P(), P(CLS))
    return jax.shard_map(
        local,
        mesh=finer,
        in_specs=placed,
        out_specs=(P(DP, CLS, None), P(CLS, DP)),
        check_vma=False,
    )
```

time: 355 us -> 105 us (0.30)
  the two profiles are of different devices: /device:TPU:8 before, /device:TPU:1 now
where the time goes in v1:
time: 105 us
  Pallas kernels  102 us (97%)
  local copies, waits for them, and re-layouts  2.67 us (3%)
    pallas_call x1, Pallas kernels, local(): pl.pallas_call(gather_kernel, out_shape=(jax.ShapeDtypeStruct((4, 5, 128,...  51.5 us
    pallas_call x1, Pallas kernels, local(): pl.pallas_call(reduce_kernel, out_shape=(jax.ShapeDtypeStruct((5, 16, 512...  50.4 us
    unnamed x2, local copies, waits for them, and re-layouts  2.67 us

profile of v1, /device:TPU:1, one launch (start us, length us, event | category | flops | bytes accessed | tf_op | source)
XLA Modules:
  0.0 105.3 jit_solution(11769394665756011511)
XLA Ops:
  0.6 51.5 %gather.1 = (s16[4,5,128,512]{3,2,1,0:T(8,128)(2,1)}, f32[8,128]{1,0:T(8,128)}, f32[8,512]{1,0:T(8,128)}) custom-call(bf16[64,4096]{1,0:T(8,128)(2,1)} %feat.1, bf16[1,512]{1,0:T(2,128)(2,1)} %coeffs.3, s32[32,128]{1,0:T(8,128)} %bitcast.3, s32[5]{0:T(128)} %slots.3), custom_call_target="tpu_custom_call" | custom-call | tf_op jit(solution)/shard_map/gather/pallas_call | solution.py:431
  52.1 50.4 %reduce.1 = (f32[5,16,512]{2,1,0:T(8,128)}, f32[1,16]{1,0:T(1,128)}) custom-call(s16[4,5,128,512]{3,2,1,0:T(8,128)(2,1)} %get-tuple-element.7.part, f32[8,128]{1,0:T(8,128)} %get-tuple-element.8.scales, f32[8,512]{1,0:T(8,128)} %get-tuple-element.9.grad, bf16[1,512]{1,0:T(2,128)(2,1)} %coeffs.3, s32[5]{0:T(128)} %slots.3, f32[8]{0:T(128)} %smoothing.1), custom_call_target="tpu_custom_call" | custom-call | tf_op jit(solution)/shard_map/reduce/pallas_call | solution.py:458
  102.6 1.6 %copy.9 = f32[16,5,512]{2,0,1:T(8,128)} copy(f32[16,5,512]{2,0,1:T(8,128)} %bitcast.2) | data formatting | bytes 327680
  104.2 1.1 %copy.10 = f32[1,16]{1,0:T(1,128)} copy(f32[1,16]{1,0:T(1,128)} %get-tuple-element.15) | data formatting | bytes 128

commit v2 on v1

v2 whole, which is shorter than its diff:
```python
import jax
import jax.numpy as jnp
from jax import lax
from jax.experimental import pallas as pl
from jax.experimental.pallas import tpu as pltpu
from jax.sharding import Mesh
from jax.sharding import PartitionSpec as P

CLASSES = 8
PAIRS = CLASSES * (CLASSES + 1) // 2
STARTS = (8, 15, 21, 26, 30, 33, 35)
DIAGONAL = (0, 8, 15, 21, 26, 30, 33, 35)
AXES = ("zl", "x", "core", "y", "zh")
DP = ("zl", "x", "core")
CLS = ("y", "zh")
MESH = pl.DeviceIdType.MESH
STEPS = 8
LEVELS = 32767.0
F32 = jnp.float32
BF16 = jnp.bfloat16


def place():
    return {name: lax.axis_index(name) for name in AXES}


def remote(src, dst, send, recv, device):
    return pltpu.make_async_remote_copy(
        src_ref=src, dst_ref=dst, send_sem=send, recv_sem=recv, device_id=device, device_id_type=MESH
    )


def pair_weights(slots, probs):
    pair = jnp.minimum(slots, PAIRS - 1)
    first = jnp.zeros_like(pair)
    start = jnp.zeros_like(pair)
    for before, at in zip((0,) + STARTS, STARTS):
        later = pair >= at
        first += jnp.where(later, 1, 0)
        start += jnp.where(later, at - before, 0)
    second = pair - start + first
    live = (slots < PAIRS)[:, :1]
    first, second = first[:, :1], second[:, :1]
    prob_first = jnp.zeros_like(probs)
    prob_second = jnp.zeros_like(probs)
    for k in range(CLASSES):
        row = probs[k : k + 1, :]
        prob_first += jnp.where(first == k, row, 0.0)
        prob_second += jnp.where(second == k, row, 0.0)
    same = jnp.where(first == second, 1.0, 0.0)
    return jnp.where(live, prob_first * (same - prob_second), 0.0)


def newton_kernel(
    feat, coeffs, labels, slots, smoothing,
    hess_out, grad_out,
    held, sent, total, labs, pairs, tiles, matrix, gsum, scales,
    relay_q, direct_q, joint_q, got_relay, got_direct, got_joint, grads,
    coded, small, far, far_small, pen_row, stage,
    own_sem, away_sem, z_send, z_recv, yo_send, yz_send, y_recv, op_send, op_recv, d_send, d_recv,
    tz_sem, ty_send, ty_recv, p_sem, l_sem, s_send, s_recv, q_send, relay_recv, direct_recv, joint_recv,
    g_send, g_recv, f_send, f_recv, fs_send, fs_recv,
):
    at = place()
    k, x, y, h, zl = at["core"], at["x"], at["y"], at["zh"], at["zl"]
    z = h * 4 + zl
    cls = y * 2 + h
    half = held.shape[3]
    rows = feat.shape[0]
    kept = feat.shape[1] // 2
    up, down, across = lax.rem(y + 1, 4), lax.rem(y + 3, 4), lax.rem(y + 2, 4)
    antipode, partner = {"zh": 1 - h}, {"core": 1 - k}

    peers = [{"x": lax.rem(x + j, 4)} for j in range(1, 4)] + [{"y": lax.rem(y + j, 4)} for j in range(1, 4)]
    for a in range(2):
        for i in range(4):
            for e in range(2):
                if a or i or e:
                    peers.append({"zl": lax.rem(zl + i, 4), "zh": lax.rem(h + a, 2), "core": lax.rem(k + e, 2)})
    barrier = pltpu.get_barrier_semaphore()
    for device in peers[::-1]:
        pl.semaphore_signal(barrier, inc=1, device_id=device, device_id_type=MESH)

    def band(q, first, size):
        return held.at[q, k, pl.ds(pl.multiple_of(first, 64), size)]

    def columns(side, q):
        return feat.at[:, pl.ds(pl.multiple_of(side * kept + q * half, half), half)]

    for q in range(STEPS):
        pltpu.make_async_copy(columns(1 - h, q), sent.at[q], away_sem.at[0]).start()
        pltpu.make_async_copy(columns(h, q), band(q, cls * rows, rows), own_sem.at[0]).start()
    label_rows = kept // 128
    own_labels = labels.at[pl.ds(pl.multiple_of(h * label_rows, 8), label_rows)]
    label_copy = pltpu.make_async_copy(own_labels, labs.at[k], l_sem.at[0])
    label_copy.start()

    row8 = lax.broadcasted_iota(jnp.int32, (8, 128), 0)
    mine = jnp.full((8, 128), 40, jnp.int32)
    for s in range(5):
        mine = jnp.where(row8 == s, slots[s], mine)
    pairs[h] = mine
    coeff_row = coeffs[...].astype(F32)
    pieces = [coeff_row[:, 128 * j : 128 * (j + 1)] for j in range(4)]
    tiles[cls] = jnp.concatenate(pieces + [jnp.zeros((4, 128), F32)], axis=0)

    total[...] = jnp.zeros_like(total)
    gsum[...] = jnp.zeros_like(gsum)
    lane = lax.broadcasted_iota(jnp.int32, (8, 512), 1)
    wide_row = jnp.broadcast_to(coeff_row, (8, 512))
    diff = wide_row - 2.0 * pltpu.roll(wide_row, 511, 1) + pltpu.roll(wide_row, 510, 1)
    diff = jnp.where(lane < 510, diff, 0.0)
    pen_row[...] = diff - 2.0 * pltpu.roll(diff, 1, 1) + pltpu.roll(diff, 2, 1)

    label_copy.wait()
    pltpu.make_async_copy(sent, sent, away_sem.at[0]).wait()
    pltpu.make_async_copy(held.at[0, 0], held.at[0, 0], own_sem.at[0]).wait()
    pl.semaphore_wait(barrier, len(peers))

    def z_copy(q, c):
        return remote(sent.at[q], band(q, c * rows, rows), z_send.at[0], z_recv.at[q], antipode)

    def y_copy(q, d, c, send):
        block = band(q, c * rows, rows)
        return remote(block, block, send.at[d], y_recv.at[d, q], {"y": (up, down)[d]})

    def op_copy(q, source):
        block = band(q, source * 2 * rows, 2 * rows)
        to = {"y": jnp.where(lax.rem(q, 2) == 0, up, down)}
        return remote(block, block, op_send.at[0], op_recv.at[q], to)

    def d_copy(q, source, count):
        block = band(q, source * 2 * rows, 2 * rows * count)
        return remote(block, block, d_send.at[0], d_recv.at[q], partner)

    def tz_copy(c):
        return remote(tiles.at[c], tiles.at[c], tz_sem.at[0], tz_sem.at[1], antipode)

    def ty_copy(j, source):
        block = tiles.at[pl.ds(source * 2, 2)]
        return remote(block, block, ty_send.at[j], ty_recv.at[4 - j], {"y": lax.rem(y + j, 4)})

    def pair_copy(side):
        return remote(pairs.at[side], pairs.at[side], p_sem.at[0], p_sem.at[1], antipode)

    def label_send(core):
        return remote(labs.at[core], labs.at[core], l_sem.at[1], l_sem.at[2], partner)

    tz_copy(cls).start()
    pair_copy(h).start()
    for q in range(STEPS):
        z_copy(q, cls).start()
        for d in range(2):
            y_copy(q, d, cls, yo_send).start()
    label_send(k).start()
    tz_copy(y * 2 + 1 - h).wait_recv()
    for j in range(1, 4):
        ty_copy(j, y).start()

    def stage_a(q):
        other = y * 2 + 1 - h
        z_copy(q, other).wait_recv()
        for d in range(2):
            y_copy(q, d, other, yz_send).start()
        d_copy(q, y, 1).start()

    def stage_b(q):
        for d, source in ((0, down), (1, up)):
            block = band(q, source * 2 * rows, 2 * rows)
            remote(block, block, yo_send.at[d], y_recv.at[d, q], {"y": (up, down)[d]}).wait_recv()
        op_copy(q, jnp.where(lax.rem(q, 2) == 0, down, up)).start()
        d_copy(q, down, 1).start()
        d_copy(q, up, 1).start()

    def stage_c(q):
        op_copy(q, across).wait_recv()
        d_copy(q, across, 1).start()

    contract = (((1,), (1,)), ((), ()))

    def prepare(q):
        theirs = held.at[q, 1 - k]
        remote(theirs, theirs, d_send.at[0], d_recv.at[q], partner).wait_recv()
        weights = []
        for core in range(2):
            block = held[q, core]
            scores = jnp.dot(matrix[...].astype(BF16), block, preferred_element_type=F32)
            exponent = jnp.exp(scores - jnp.max(scores, axis=0, keepdims=True))
            probs = exponent / jnp.sum(exponent, axis=0, keepdims=True)
            weights.append(pair_weights(pairs[k], probs))
            lab_rows = [labs[core, pl.ds(q * (half // 128) + i, 1), :] for i in range(half // 128)]
            lab = jnp.concatenate(lab_rows, axis=1)
            one_hot = lax.broadcasted_iota(jnp.int32, (8, half), 0) == lab
            resid = (jnp.where(one_hot, 1.0, 0.0) - probs).astype(BF16)
            gsum[...] += lax.dot_general(resid, block, contract, preferred_element_type=F32)
        return weights

    def add_products(q, s, weights):
        term = None
        for core in range(2):
            block = held[q, core]
            scaled = (block.astype(F32) * weights[core][s : s + 1, :]).astype(BF16)
            product = lax.dot_general(scaled, block, contract, preferred_element_type=F32)
            term = product if term is None else term + product
        total[s] += term.reshape(4, 4, 32, 512)

    def step(t, carry):
        @pl.when(t < STEPS)
        def _():
            stage_a(t)

        @pl.when((t >= 1) & (t < STEPS + 1))
        def _():
            stage_b(t - 1)

        @pl.when(t >= 2)
        def _():
            stage_c(t - 2)

        @pl.when(t == 3)
        def _():
            for j in range(1, 4):
                ty_copy(4 - j, lax.rem(y + 4 - j, 4)).wait_recv()
            pair_copy(1 - h).wait_recv()
            label_send(1 - k).wait_recv()
            for c in range(CLASSES):
                tile = tiles[c]
                matrix[c : c + 1, :] = jnp.concatenate([tile[j : j + 1, :] for j in range(4)], axis=1)

        @pl.when(t >= 3)
        def _():
            weights = prepare(t - 3)
            for s in range(5):
                add_products(t - 3, s, weights)

        return carry

    lax.fori_loop(0, STEPS + 2, step, 0)

    def turn(s):
        ahead = lax.rem(k + s, 2) == 0
        return jnp.where(ahead, 1, 3), jnp.where(ahead, 3, 1)

    def around(j):
        return lax.rem(x + j, 4)

    def s_copy(s, j, source):
        tile = scales.at[source, s]
        return remote(tile, tile, s_send.at[0], s_recv.at[4 - j, s], {"x": around(j)})

    def relay_copy(s):
        return remote(relay_q.at[s], got_relay.at[s], q_send.at[0], relay_recv.at[s], {"x": around(turn(s)[0])})

    def direct_copy(s):
        return remote(direct_q.at[s], got_direct.at[s], q_send.at[1], direct_recv.at[s], {"x": around(turn(s)[1])})

    def joint_copy(s):
        return remote(joint_q.at[s], got_joint.at[s], q_send.at[2], joint_recv.at[s], {"x": around(turn(s)[0])})

    def g_copy(j, source):
        return remote(grads.at[source], grads.at[source], g_send.at[0], g_recv.at[4 - j], {"x": around(j)})

    def largest_of(block):
        top = jnp.max(jnp.max(jnp.abs(block), axis=0, keepdims=True), axis=1, keepdims=True)
        return jnp.maximum(top, 1e-30)

    def piece(s, j):
        return total[s, :, pl.ds(around(j), 1)].reshape(128, 512)

    def code(block, inverse):
        return jnp.round(block * inverse).astype(jnp.int32).astype(jnp.int16)

    def plain(block):
        return block.astype(jnp.int32).astype(F32)

    def scale_of(j, s):
        return scales[around(j), s, 0:1, 0:1]

    def first_sums(s, weights):
        add_products(STEPS - 1, s, weights)
        top = largest_of(total[s].reshape(512, 512))
        scales[x, s] = jnp.broadcast_to(top * (1.0 / LEVELS), (8, 128))
        inverse = LEVELS / top
        relay_q[s] = code(piece(s, 2), inverse)
        for j in (1, 3, 2):
            s_copy(s, j, x).start()
        relay_copy(s).start()
        direct_q[s] = code(piece(s, turn(s)[1]), inverse)
        direct_copy(s).start()

    def s_wait(s, j):
        tile = scales.at[around(j), s]
        remote(tile, tile, s_send.at[0], s_recv.at[j, s], {"x": around(j)}).wait_recv()

    def joint_sums(s):
        ahead, behind = turn(s)
        relay_copy(s).wait_recv()
        s_wait(s, behind)
        scale, own = scale_of(behind, s), scale_of(0, s)
        value = plain(got_relay[s]) * scale + piece(s, ahead)
        joint_q[s] = code(value, 1.0 / (scale + own))
        joint_copy(s).start()

    def owner(i, e):
        return {"zl": lax.rem(zl + i, 4), "zh": k, "core": lax.rem(k + e, 2)}

    def f_copy(s, i, e):
        src = coded.at[s, lax.rem(zl + i, 4), lax.rem(k + e, 2)]
        return remote(src, far.at[s, z], f_send.at[i, e], f_recv.at[s], owner(i, e))

    def fs_copy(i, e):
        src = small.at[lax.rem(zl + i, 4)]
        return remote(src, far_small.at[z], fs_send.at[i, e], fs_recv.at[0], owner(i, e))

    def to_owners(act):
        for i in (2, 1, 3, 0):
            for e in range(2):
                if i or e:
                    act(i, e)
                else:
                    pl.when(h != k)(lambda: act(0, 0))

    def last_sums(s):
        ahead, behind = turn(s)
        joint_copy(s).wait_recv()
        direct_copy(s).wait_recv()
        s_wait(s, ahead)
        s_wait(s, 2)
        value = piece(s, 0) + plain(got_joint[s]) * (scale_of(behind, s) + scale_of(2, s))
        value += plain(got_direct[s]) * scale_of(ahead, s)
        top = largest_of(value)
        out = code(value, LEVELS / top)
        for i in range(4):
            for e in range(2):
                first = i * 32 + e * 16
                coded[s, i, e] = out[first : first + 16, :]
        to_owners(lambda i, e: f_copy(s, i, e).start())
        pl.when(h == k)(lambda: pltpu.make_async_copy(coded.at[s, zl, k], far.at[s, z], f_recv.at[s]).start())
        return top * (1.0 / LEVELS)

    scale2 = jnp.zeros((8, 128), F32)
    weights = prepare(STEPS - 1)
    grads[x] = gsum[...]
    for j in (1, 3, 2):
        g_copy(j, x).start()
    for t in range(5 + 2):
        if t < 5:
            first_sums(t, weights)
        if 1 <= t < 6:
            joint_sums(t - 1)
        if t >= 2:
            scale2 = jnp.where(row8 == t - 2, last_sums(t - 2), scale2)

    for j in (1, 3, 2):
        g_copy(4 - j, around(4 - j)).wait_recv()
    all_grad = grads[0] + grads[1] + grads[2] + grads[3]
    for i in range(4):
        small[i, 0] = all_grad[:, 128 * i : 128 * (i + 1)]
        small[i, 1] = scale2
    to_owners(lambda i, e: fs_copy(i, e).start())
    pl.when(h == k)(lambda: pltpu.make_async_copy(small.at[zl], far_small.at[z], fs_recv.at[0]).start())

    row0 = zl * 128 + x * 32 + k * 16
    ia = lax.broadcasted_iota(jnp.int32, (16, 512), 0) + row0
    ib = lax.broadcasted_iota(jnp.int32, (16, 512), 1)
    pen = jnp.zeros((16, 512), F32)
    taps = (1.0, -2.0, 1.0)
    for m in range(3):
        inside = (ia - m >= 0) & (ia - m <= 509)
        for n in range(3):
            pen += jnp.where(inside & (ib - n == ia - m), taps[m] * taps[n], 0.0)

    pltpu.make_async_copy(far_small, far_small, fs_recv.at[0]).wait()
    summed = far_small[0, 0]
    for source in range(1, 8):
        summed += far_small[source, 0]
    picked = jnp.sum(jnp.where(row8 == cls, summed, 0.0), axis=0, keepdims=True) * (1.0 / 4096.0)
    pen_part = pen_row[:, pl.ds(pl.multiple_of(zl * 128, 128), 128)]
    final = picked - smoothing[cls] * pen_part
    stage[...] = pltpu.roll(final, lax.rem(128 - (x * 32 + k * 16), 128), 1)
    grad_out[...] = stage[0:1, 0:16]
    for s in range(5):
        pltpu.make_async_copy(far.at[s], far.at[s], f_recv.at[s]).wait()
        value = jnp.zeros((16, 512), F32)
        for source in range(8):
            value += plain(far[s, source]) * far_small[source, 1, s : s + 1, 0:1]
        smooth = jnp.float32(0.0)
        for j, number in enumerate(DIAGONAL):
            smooth += jnp.where(slots[s] == number, smoothing[j], 0.0)
        hess_out[s] = value * (1.0 / 4096.0) + pen * smooth

    def sent_all(ref, sem):
        pltpu.make_async_copy(ref, ref, sem).wait()

    tz_copy(cls).wait_send()
    pair_copy(h).wait_send()
    label_send(k).wait_send()
    for j in range(1, 4):
        ty_copy(j, y).wait_send()
    sent_all(sent, z_send.at[0])
    for d in range(2):
        sent_all(held.at[0, 0], yo_send.at[d])
        sent_all(held.at[0, 0], yz_send.at[d])
    sent_all(held.at[0], op_send.at[0])
    sent_all(held.at[pl.ds(0, STEPS // 2)], d_send.at[0])
    sent_all(scales.at[pl.ds(0, 3)], s_send.at[0])
    for i in range(3):
        sent_all(relay_q, q_send.at[i])
    sent_all(grads.at[pl.ds(0, 3)], g_send.at[0])
    to_owners(lambda i, e: sent_all(coded.at[:, 0, 0], f_send.at[i, e]))
    to_owners(lambda i, e: fs_copy(i, e).wait_send())


def local(features, labels, coeffs, smoothing, pair_slots):
    vmem = pl.BlockSpec(memory_space=pltpu.VMEM)
    smem = pl.BlockSpec(memory_space=pltpu.SMEM)
    anyspace = pl.BlockSpec(memory_space=pl.ANY)
    dma = pltpu.SemaphoreType.DMA
    half = features.shape[1] // 2 // STEPS
    block = pltpu.VMEM((5, 128, 512), jnp.int16)
    hessian, gradient = pl.pallas_call(
        newton_kernel,
        out_shape=(
            jax.ShapeDtypeStruct((5, 16, 512), F32),
            jax.ShapeDtypeStruct((1, 16), F32),
        ),
        in_specs=[anyspace, vmem, anyspace, smem, smem],
        out_specs=(vmem, vmem),
        scratch_shapes=[
            pltpu.VMEM((STEPS, 2, 512, half), BF16),
            pltpu.VMEM((STEPS, 64, half), BF16),
            pltpu.VMEM((5, 4, 4, 32, 512), F32),
            pltpu.VMEM((2, 16, 128), jnp.int32),
            pltpu.VMEM((2, 8, 128), jnp.int32),
            pltpu.VMEM((8, 8, 128), F32),
            pltpu.VMEM((8, 512), F32),
            pltpu.VMEM((8, 512), F32),
            pltpu.VMEM((4, 5, 8, 128), F32),
            block, block, block, block, block, block,
            pltpu.VMEM((4, 8, 512), F32),
            pltpu.VMEM((5, 4, 2, 16, 512), jnp.int16),
            pltpu.VMEM((4, 2, 8, 128), F32),
            pltpu.VMEM((5, 8, 16, 512), jnp.int16),
            pltpu.VMEM((8, 2, 8, 128), F32),
            pltpu.VMEM((8, 512), F32),
            pltpu.VMEM((8, 128), F32),
            dma((1,)), dma((1,)), dma((1,)), dma((STEPS,)), dma((2,)), dma((2,)), dma((2, STEPS)),
            dma((1,)), dma((STEPS,)), dma((1,)), dma((STEPS,)),
            dma((2,)), dma((4,)), dma((4,)), dma((2,)), dma((3,)),
            dma((1,)), dma((4, 5)), dma((3,)), dma((5,)), dma((5,)), dma((5,)),
            dma((1,)), dma((4,)), dma((4, 2)), dma((5,)), dma((4, 2)), dma((1,)),
        ],
        compiler_params=pltpu.CompilerParams(collective_id=0, has_side_effects=True),
        name="newton",
    )(features, coeffs, labels.reshape(32, 128), pair_slots, smoothing)
    return hessian.transpose(1, 0, 2), gradient


def solution(mesh):
    finer = Mesh(mesh.devices.reshape(4, 4, 2, 4, 2), AXES)
    placed = (P(CLS, DP), P(DP), P(CLS, None), P(), P(CLS))
    return jax.shard_map(
        local,
        mesh=finer,
        in_specs=placed,
        out_specs=(P(DP, CLS, None), P(CLS, DP)),
        check_vma=False,
    )
```

time: 105 us -> 86.7 us (0.83)
  Pallas kernels: 102 us -> 83.8 us
    pallas_call x2 -> x1, Pallas kernels: 102 us -> 83.8 us  [local(): pl.pallas_call(newton_kernel, out_shape=(jax.ShapeDtypeStruct((5, 16, 512...]
    unnamed x2 -> x4, local copies, waits for them, and re-layouts: 2.67 us -> 2.11 us
where the time goes in v2:
time: 86.7 us; the launch traced here: 86.5 us
  Pallas kernels  83.8 us (97%)
  local copies, waits for them, and re-layouts  2.11 us (2%)
    pallas_call x1, Pallas kernels, local(): pl.pallas_call(newton_kernel, out_shape=(jax.ShapeDtypeStruct((5, 16, 512...  83.8 us
    unnamed x4, local copies, waits for them, and re-layouts  2.11 us

profile of v2, /device:TPU:1, one launch (start us, length us, event | category | flops | bytes accessed | tf_op | source)
XLA Modules:
  0.0 86.5 jit_solution(13422638305494903027)
XLA Ops:
  0.6 83.8 %newton.1 = (f32[5,16,512]{2,1,0:T(8,128)}, f32[1,16]{1,0:T(1,128)}) custom-call(bf16[64,4096]{1,0:T(8,128)(2,1)} %feat.1, bf16[1,512]{1,0:T(2,128)(2,1)} %coeffs.1, s32[32,128]{1,0:T(8,128)} %bitcast.3, s32[5]{0:T(128)} %slots.1, f32[8]{0:T(128)} %smoothing.1), custom_call_target="tpu_custom_call" | custom-call | tf_op jit(solution)/shard_map/newton/pallas_call | solution.py:421
  84.4 0.0 copy-start
  84.4 1.6 %copy.9 = f32[16,5,512]{2,0,1:T(8,128)} copy(f32[16,5,512]{2,0,1:T(8,128)} %bitcast.2) | data formatting | bytes 327680
  86.0 0.0 copy-done
  86.0 0.5 copy.10
Async XLA Ops:
  84.4 1.6 %copy-start = (f32[1,16]{1,0:T(1,128)S(1)}, f32[1,16]{1,0:T(1,128)}, u32[]{:S(2)}) copy-start(f32[1,16]{1,0:T(1,128)} %get-tuple-element.9) | copy-start | bytes 196

commit v3 on v2

--- a/solution.py
+++ b/solution.py
@@ -16,6 +16,10 @@
 MESH = pl.DeviceIdType.MESH
 STEPS = 8
 LEVELS = 32767.0
+ORDER = (
+    ("beta", 4), ("first", 0), ("first", 1), ("joint", 0), ("first", 2), ("joint", 1), ("last", 0), ("first", 3),
+    ("joint", 2), ("last", 1), ("joint", 3), ("last", 2), ("cross", 4), ("last", 3),
+)
 F32 = jnp.float32
 BF16 = jnp.bfloat16
 
@@ -54,12 +58,12 @@
 def newton_kernel(
     feat, coeffs, labels, slots, smoothing,
     hess_out, grad_out,
-    held, sent, total, labs, pairs, tiles, matrix, gsum, scales,
+    held, sent, total, labs, pairs, tiles, matrix, factors, resids, gsum, scales,
     relay_q, direct_q, joint_q, got_relay, got_direct, got_joint, grads,
-    coded, small, far, far_small, pen_row, stage,
+    coded, small, far, far_small, b_q, b_scale, far_b, far_bs, b_sum, got_b, pen_row, stage,
     own_sem, away_sem, z_send, z_recv, yo_send, yz_send, y_recv, op_send, op_recv, d_send, d_recv,
     tz_sem, ty_send, ty_recv, p_sem, l_sem, s_send, s_recv, q_send, relay_recv, direct_recv, joint_recv,
-    g_send, g_recv, f_send, f_recv, fs_send, fs_recv,
+    g_send, g_recv, f_send, f_recv, fs_send, fs_recv, b_send, b_recv, bs_send, bs_recv, bx_send, bx_recv,
 ):
     at = place()
     k, x, y, h, zl = at["core"], at["x"], at["y"], at["zh"], at["zl"]
@@ -178,64 +182,75 @@
 
     contract = (((1,), (1,)), ((), ()))
 
-    def prepare(q):
+    def wait_partner(q):
         theirs = held.at[q, 1 - k]
         remote(theirs, theirs, d_send.at[0], d_recv.at[q], partner).wait_recv()
-        weights = []
+
+    def prepare(q):
+        both = [jnp.dot(matrix[...].astype(BF16), held[q, core], preferred_element_type=F32) for core in range(2)]
+        scores = jnp.concatenate(both, axis=1)
+        exponent = jnp.exp(scores - jnp.max(scores, axis=0, keepdims=True))
+        probs = exponent / jnp.sum(exponent, axis=0, keepdims=True)
+        turn = lax.rem(q, 2)
+        factors[turn] = pair_weights(pairs[k], probs)
+        lab_rows = [
+            labs[core, pl.ds(q * (half // 128) + i, 1), :] for core in range(2) for i in range(half // 128)
+        ]
+        lab = jnp.concatenate(lab_rows, axis=1)
+        one_hot = lax.broadcasted_iota(jnp.int32, (8, 2 * half), 0) == lab
+        resids[turn] = jnp.where(one_hot, 1.0, 0.0) - probs
+
+    def add_products(q, s):
+        turn = lax.rem(q, 2)
+        left, right, extra = None, None, None
         for core in range(2):
             block = held[q, core]
-            scores = jnp.dot(matrix[...].astype(BF16), block, preferred_element_type=F32)
-            exponent = jnp.exp(scores - jnp.max(scores, axis=0, keepdims=True))
-            probs = exponent / jnp.sum(exponent, axis=0, keepdims=True)
-            weights.append(pair_weights(pairs[k], probs))
-            lab_rows = [labs[core, pl.ds(q * (half // 128) + i, 1), :] for i in range(half // 128)]
-            lab = jnp.concatenate(lab_rows, axis=1)
-            one_hot = lax.broadcasted_iota(jnp.int32, (8, half), 0) == lab
-            resid = (jnp.where(one_hot, 1.0, 0.0) - probs).astype(BF16)
-            gsum[...] += lax.dot_general(resid, block, contract, preferred_element_type=F32)
-        return weights
-
-    def add_products(q, s, weights):
-        term = None
-        for core in range(2):
-            block = held[q, core]
-            scaled = (block.astype(F32) * weights[core][s : s + 1, :]).astype(BF16)
-            product = lax.dot_general(scaled, block, contract, preferred_element_type=F32)
-            term = product if term is None else term + product
-        total[s] += term.reshape(4, 4, 32, 512)
+            span = slice(core * half, (core + 1) * half)
+            scaled = (block.astype(F32) * factors[turn, s : s + 1, span]).astype(BF16)
+            first = lax.dot_general(scaled[:256], block[:256], contract, preferred_element_type=F32)
+            second = lax.dot_general(scaled, block[256:], contract, preferred_element_type=F32)
+            left = first if left is None else left + first
+            right = second if right is None else right + second
+            if s == 0:
+                resid = resids[turn, :, span].astype(BF16)
+                term = lax.dot_general(resid, block, contract, preferred_element_type=F32)
+                extra = term if extra is None else extra + term
+        total[s, 0:2, :, :, 0:256] += left.reshape(2, 4, 32, 256)
+        total[s, :, :, :, 256:512] += right.reshape(4, 4, 32, 256)
+        if s == 0:
+            gsum[...] += extra
+
+    for t in range(6):
+        stage_a(t)
+        if t >= 2:
+            stage_b(t - 2)
+        if t >= 4:
+            stage_c(t - 4)
+    for j in range(1, 4):
+        ty_copy(4 - j, lax.rem(y + 4 - j, 4)).wait_recv()
+    pair_copy(1 - h).wait_recv()
+    label_send(1 - k).wait_recv()
+    for c in range(CLASSES):
+        tile = tiles[c]
+        matrix[c : c + 1, :] = jnp.concatenate([tile[j : j + 1, :] for j in range(4)], axis=1)
+    wait_partner(0)
+    prepare(0)
 
     def step(t, carry):
-        @pl.when(t < STEPS)
-        def _():
-            stage_a(t)
-
-        @pl.when((t >= 1) & (t < STEPS + 1))
-        def _():
-            stage_b(t - 1)
-
-        @pl.when(t >= 2)
-        def _():
-            stage_c(t - 2)
-
-        @pl.when(t == 3)
-        def _():
-            for j in range(1, 4):
-                ty_copy(4 - j, lax.rem(y + 4 - j, 4)).wait_recv()
-            pair_copy(1 - h).wait_recv()
-            label_send(1 - k).wait_recv()
-            for c in range(CLASSES):
-                tile = tiles[c]
-                matrix[c : c + 1, :] = jnp.concatenate([tile[j : j + 1, :] for j in range(4)], axis=1)
-
-        @pl.when(t >= 3)
-        def _():
-            weights = prepare(t - 3)
-            for s in range(5):
-                add_products(t - 3, s, weights)
-
+        for stage, first in ((stage_a, 6), (stage_b, 4), (stage_c, 2)):
+
+            @pl.when(t < STEPS - first)
+            def _():
+                stage(t + first)
+
+        wait_partner(t + 1)
+        for s in range(5):
+            add_products(t, s)
+            if s == 0:
+                prepare(t + 1)
         return carry
 
-    lax.fori_loop(0, STEPS + 2, step, 0)
+    lax.fori_loop(0, STEPS - 1, step, 0)
 
     def turn(s):
         ahead = lax.rem(k + s, 2) == 0
@@ -276,8 +291,13 @@
     def scale_of(j, s):
         return scales[around(j), s, 0:1, 0:1]
 
-    def first_sums(s, weights):
-        add_products(STEPS - 1, s, weights)
+    def finish(s):
+        add_products(STEPS - 1, s)
+        corner = total[s, 0:2, :, :, 256:512].reshape(256, 256)
+        total[s, 2:4, :, :, 0:256] = corner.T.reshape(2, 4, 32, 256)
+
+    def first_sums(s):
+        finish(s)
         top = largest_of(total[s].reshape(512, 512))
         scales[x, s] = jnp.broadcast_to(top * (1.0 / LEVELS), (8, 128))
         inverse = LEVELS / top
@@ -326,8 +346,8 @@
         direct_copy(s).wait_recv()
         s_wait(s, ahead)
         s_wait(s, 2)
-        value = piece(s, 0) + plain(got_joint[s]) * (scale_of(behind, s) + scale_of(2, s))
-        value += plain(got_direct[s]) * scale_of(ahead, s)
+        value = piece(s, 0) + plain(got_direct[s]) * scale_of(ahead, s)
+        value += plain(got_joint[s]) * (scale_of(behind, s) + scale_of(2, s))
         top = largest_of(value)
         out = code(value, LEVELS / top)
         for i in range(4):
@@ -338,18 +358,59 @@
         pl.when(h == k)(lambda: pltpu.make_async_copy(coded.at[s, zl, k], far.at[s, z], f_recv.at[s]).start())
         return top * (1.0 / LEVELS)
 
+    def b_copy(i, e):
+        src = b_q.at[lax.rem(zl + i, 4), lax.rem(k + e, 2)]
+        return remote(src, far_b.at[z], b_send.at[i, e], b_recv.at[0], owner(i, e))
+
+    def bs_copy(i, e):
+        return remote(b_scale, far_bs.at[z], bs_send.at[i, e], bs_recv.at[0], owner(i, e))
+
+    def bx_copy(j, source):
+        return remote(b_sum.at[around(j)], got_b.at[source], bx_send.at[0], bx_recv.at[4 - j], {"x": around(j)})
+
+    def beta_sums(s):
+        finish(s)
+        top = largest_of(total[s].reshape(512, 512))
+        b_scale[...] = jnp.broadcast_to(top * (1.0 / LEVELS), (8, 128))
+        inverse = LEVELS / top
+        for i in range(4):
+            for c in range(2):
+                for p in range(4):
+                    b_q[i, c, 16 * p : 16 * (p + 1), :] = code(total[s, i, p, 16 * c : 16 * (c + 1), :], inverse)
+        to_owners(lambda i, e: b_copy(i, e).start())
+        to_owners(lambda i, e: bs_copy(i, e).start())
+
+        @pl.when(h == k)
+        def _():
+            pltpu.make_async_copy(b_q.at[zl, k], far_b.at[z], b_recv.at[0]).start()
+            pltpu.make_async_copy(b_scale, far_bs.at[z], bs_recv.at[0]).start()
+
+    def cross_sums():
+        pltpu.make_async_copy(far_b, far_b, b_recv.at[0]).wait()
+        pltpu.make_async_copy(far_bs, far_bs, bs_recv.at[0]).wait()
+        value = jnp.zeros((64, 512), F32)
+        for source in range(8):
+            value += plain(far_b[source]) * far_bs[source, 0:1, 0:1]
+        b_sum[...] = value.reshape(4, 16, 512)
+        for j in (1, 3, 2):
+            bx_copy(j, x).start()
+
     scale2 = jnp.zeros((8, 128), F32)
-    weights = prepare(STEPS - 1)
-    grads[x] = gsum[...]
-    for j in (1, 3, 2):
-        g_copy(j, x).start()
-    for t in range(5 + 2):
-        if t < 5:
-            first_sums(t, weights)
-        if 1 <= t < 6:
-            joint_sums(t - 1)
-        if t >= 2:
-            scale2 = jnp.where(row8 == t - 2, last_sums(t - 2), scale2)
+    for act, s in ORDER:
+        if act == "beta":
+            beta_sums(s)
+        if act == "cross":
+            cross_sums()
+        if act == "first":
+            first_sums(s)
+            if s == 0:
+                grads[x] = gsum[...]
+                for j in (1, 3, 2):
+                    g_copy(j, x).start()
+        if act == "joint":
+            joint_sums(s)
+        if act == "last":
+            scale2 = jnp.where(row8 == s, last_sums(s), scale2)
 
     for j in (1, 3, 2):
         g_copy(4 - j, around(4 - j)).wait_recv()
@@ -380,10 +441,16 @@
     stage[...] = pltpu.roll(final, lax.rem(128 - (x * 32 + k * 16), 128), 1)
     grad_out[...] = stage[0:1, 0:16]
     for s in range(5):
-        pltpu.make_async_copy(far.at[s], far.at[s], f_recv.at[s]).wait()
-        value = jnp.zeros((16, 512), F32)
-        for source in range(8):
-            value += plain(far[s, source]) * far_small[source, 1, s : s + 1, 0:1]
+        if s == 4:
+            value = b_sum[x]
+            for j in (1, 3, 2):
+                bx_copy(4 - j, around(j)).wait_recv()
+                value += got_b[around(j)]
+        else:
+            pltpu.make_async_copy(far.at[s], far.at[s], f_recv.at[s]).wait()
+            value = jnp.zeros((16, 512), F32)
+            for source in range(8):
+                value += plain(far[s, source]) * far_small[source, 1, s : s + 1, 0:1]
         smooth = jnp.float32(0.0)
         for j, number in enumerate(DIAGONAL):
             smooth += jnp.where(slots[s] == number, smoothing[j], 0.0)
@@ -404,6 +471,9 @@
     sent_all(held.at[0], op_send.at[0])
     sent_all(held.at[pl.ds(0, STEPS // 2)], d_send.at[0])
     sent_all(scales.at[pl.ds(0, 3)], s_send.at[0])
+    sent_all(got_b.at[pl.ds(0, 3)], bx_send.at[0])
+    to_owners(lambda i, e: b_copy(i, e).wait_send())
+    to_owners(lambda i, e: bs_copy(i, e).wait_send())
     for i in range(3):
         sent_all(relay_q, q_send.at[i])
     sent_all(grads.at[pl.ds(0, 3)], g_send.at[0])
@@ -417,7 +487,7 @@
     anyspace = pl.BlockSpec(memory_space=pl.ANY)
     dma = pltpu.SemaphoreType.DMA
     half = features.shape[1] // 2 // STEPS
-    block = pltpu.VMEM((5, 128, 512), jnp.int16)
+    block = pltpu.VMEM((4, 128, 512), jnp.int16)
     hessian, gradient = pl.pallas_call(
         newton_kernel,
         out_shape=(
@@ -434,21 +504,30 @@
             pltpu.VMEM((2, 8, 128), jnp.int32),
             pltpu.VMEM((8, 8, 128), F32),
             pltpu.VMEM((8, 512), F32),
+            pltpu.VMEM((2, 8, 2 * half), F32),
+            pltpu.VMEM((2, 8, 2 * half), F32),
             pltpu.VMEM((8, 512), F32),
-            pltpu.VMEM((4, 5, 8, 128), F32),
+            pltpu.VMEM((4, 4, 8, 128), F32),
             block, block, block, block, block, block,
             pltpu.VMEM((4, 8, 512), F32),
-            pltpu.VMEM((5, 4, 2, 16, 512), jnp.int16),
+            pltpu.VMEM((4, 4, 2, 16, 512), jnp.int16),
             pltpu.VMEM((4, 2, 8, 128), F32),
-            pltpu.VMEM((5, 8, 16, 512), jnp.int16),
+            pltpu.VMEM((4, 8, 16, 512), jnp.int16),
             pltpu.VMEM((8, 2, 8, 128), F32),
+            pltpu.VMEM((4, 2, 64, 512), jnp.int16),
+            pltpu.VMEM((8, 128), F32),
+            pltpu.VMEM((8, 64, 512), jnp.int16),
+            pltpu.VMEM((8, 8, 128), F32),
+            pltpu.VMEM((4, 16, 512), F32),
+            pltpu.VMEM((4, 16, 512), F32),
             pltpu.VMEM((8, 512), F32),
             pltpu.VMEM((8, 128), F32),
             dma((1,)), dma((1,)), dma((1,)), dma((STEPS,)), dma((2,)), dma((2,)), dma((2, STEPS)),
             dma((1,)), dma((STEPS,)), dma((1,)), dma((STEPS,)),
             dma((2,)), dma((4,)), dma((4,)), dma((2,)), dma((3,)),
-            dma((1,)), dma((4, 5)), dma((3,)), dma((5,)), dma((5,)), dma((5,)),
-            dma((1,)), dma((4,)), dma((4, 2)), dma((5,)), dma((4, 2)), dma((1,)),
+            dma((1,)), dma((4, 4)), dma((3,)), dma((4,)), dma((4,)), dma((4,)),
+            dma((1,)), dma((4,)), dma((4, 2)), dma((4,)), dma((4, 2)), dma((1,)),
+            dma((4, 2)), dma((1,)), dma((4, 2)), dma((1,)), dma((1,)), dma((4,)),
         ],
         compiler_params=pltpu.CompilerParams(collective_id=0, has_side_effects=True),
         name="newton",

time: 86.7 us -> 78.6 us (0.907)
  Pallas kernels: 83.8 us -> 75.6 us
    pallas_call x1, Pallas kernels: 83.8 us -> 75.6 us  [local(): pl.pallas_call(newton_kernel, out_shape=(jax.ShapeDtypeStruct((5, 16, 512...]
where the time goes in v3:
time: 78.6 us; the launch traced here: 78.4 us
  Pallas kernels  75.6 us (96%)
  local copies, waits for them, and re-layouts  2.11 us (3%)
    pallas_call x1, Pallas kernels, local(): pl.pallas_call(newton_kernel, out_shape=(jax.ShapeDtypeStruct((5, 16, 512...  75.6 us
    unnamed x4, local copies, waits for them, and re-layouts  2.11 us

profile of v3, /device:TPU:1, one launch (start us, length us, event | category | flops | bytes accessed | tf_op | source)
XLA Modules:
  0.0 78.4 jit_solution(11696083241332078094)
XLA Ops:
  0.6 75.6 %newton.1 = (f32[5,16,512]{2,1,0:T(8,128)}, f32[1,16]{1,0:T(1,128)}) custom-call(bf16[64,4096]{1,0:T(8,128)(2,1)} %feat.1, bf16[1,512]{1,0:T(2,128)(2,1)} %coeffs.1, s32[32,128]{1,0:T(8,128)} %bitcast.3, s32[5]{0:T(128)} %slots.1, f32[8]{0:T(128)} %smoothing.1), custom_call_target="tpu_custom_call" | custom-call | tf_op jit(solution)/shard_map/newton/pallas_call | solution.py:491
  76.3 0.0 copy-start
  76.3 1.6 %copy.9 = f32[16,5,512]{2,0,1:T(8,128)} copy(f32[16,5,512]{2,0,1:T(8,128)} %bitcast.2) | data formatting | bytes 327680
  77.9 0.0 copy-done
  77.9 0.5 copy.10
Async XLA Ops:
  76.3 1.6 %copy-start = (f32[1,16]{1,0:T(1,128)S(1)}, f32[1,16]{1,0:T(1,128)}, u32[]{:S(2)}) copy-start(f32[1,16]{1,0:T(1,128)} %get-tuple-element.9) | copy-start | bytes 196

commit v4 on v3

--- a/solution.py
+++ b/solution.py
@@ -15,10 +15,12 @@
 CLS = ("y", "zh")
 MESH = pl.DeviceIdType.MESH
 STEPS = 8
+AROUND = 4
 LEVELS = 32767.0
 ORDER = (
-    ("beta", 4), ("first", 0), ("first", 1), ("joint", 0), ("first", 2), ("joint", 1), ("last", 0), ("first", 3),
-    ("joint", 2), ("last", 1), ("joint", 3), ("last", 2), ("cross", 4), ("last", 3),
+    ("first", 0, 0), ("first", 1, 0), ("beta", 4, 0), ("joint", 0, 0), ("joint", 0, 1), ("first", 2, 0), ("joint", 1, 0), ("joint", 1, 1), ("first", 3, 0),
+    ("last", 0, 0), ("joint", 2, 0), ("last", 0, 1), ("joint", 2, 1), ("last", 1, 0), ("joint", 3, 0), ("last", 1, 1), ("joint", 3, 1),
+    ("last", 2, 0), ("last", 2, 1), ("cross", 4, 0), ("last", 3, 0), ("last", 3, 1),
 )
 F32 = jnp.float32
 BF16 = jnp.bfloat16
@@ -58,7 +60,7 @@
 def newton_kernel(
     feat, coeffs, labels, slots, smoothing,
     hess_out, grad_out,
-    held, sent, total, labs, pairs, tiles, matrix, factors, resids, gsum, scales,
+    held, sent, total, labs, pairs, tiles, matrix, factors, resids, later_factors, later_resids, gsum, scales,
     relay_q, direct_q, joint_q, got_relay, got_direct, got_joint, grads,
     coded, small, far, far_small, b_q, b_scale, far_b, far_bs, b_sum, got_b, pen_row, stage,
     own_sem, away_sem, z_send, z_recv, yo_send, yz_send, y_recv, op_send, op_recv, d_send, d_recv,
@@ -108,6 +110,48 @@
     pieces = [coeff_row[:, 128 * j : 128 * (j + 1)] for j in range(4)]
     tiles[cls] = jnp.concatenate(pieces + [jnp.zeros((4, 128), F32)], axis=0)
 
+    pl.semaphore_wait(barrier, len(peers))
+    pltpu.make_async_copy(sent, sent, away_sem.at[0]).wait()
+    pltpu.make_async_copy(held.at[0, 0], held.at[0, 0], own_sem.at[0]).wait()
+    label_copy.wait()
+
+    def z_copy(q, c):
+        return remote(sent.at[q], band(q, c * rows, rows), z_send.at[0], z_recv.at[q], antipode)
+
+    def y_copy(q, d, c, send):
+        block = band(q, c * rows, rows)
+        return remote(block, block, send.at[d], y_recv.at[d, q], {"y": (up, down)[d]})
+
+    def op_copy(q, source):
+        block = band(q, source * 2 * rows, 2 * rows)
+        to = {"y": jnp.where(lax.rem(q, 2) == 0, up, down)}
+        return remote(block, block, op_send.at[0], op_recv.at[q], to)
+
+    def d_copy(q, source, count):
+        block = band(q, source * 2 * rows, 2 * rows * count)
+        return remote(block, block, d_send.at[0], d_recv.at[q], partner)
+
+    def tz_copy(c):
+        return remote(tiles.at[c], tiles.at[c], tz_sem.at[0], tz_sem.at[1], antipode)
+
+    def ty_copy(j, source):
+        block = tiles.at[pl.ds(source * 2, 2)]
+        return remote(block, block, ty_send.at[j], ty_recv.at[4 - j], {"y": lax.rem(y + j, 4)})
+
+    def pair_copy(side):
+        return remote(pairs.at[side], pairs.at[side], p_sem.at[0], p_sem.at[1], antipode)
+
+    def label_send(core):
+        return remote(labs.at[core], labs.at[core], l_sem.at[1], l_sem.at[2], partner)
+
+    tz_copy(cls).start()
+    pair_copy(h).start()
+    for q in range(STEPS):
+        z_copy(q, cls).start()
+        for d in range(2):
+            y_copy(q, d, cls, yo_send).start()
+    label_send(k).start()
+
     total[...] = jnp.zeros_like(total)
     gsum[...] = jnp.zeros_like(gsum)
     lane = lax.broadcasted_iota(jnp.int32, (8, 512), 1)
@@ -116,47 +160,6 @@
     diff = jnp.where(lane < 510, diff, 0.0)
     pen_row[...] = diff - 2.0 * pltpu.roll(diff, 1, 1) + pltpu.roll(diff, 2, 1)
 
-    label_copy.wait()
-    pltpu.make_async_copy(sent, sent, away_sem.at[0]).wait()
-    pltpu.make_async_copy(held.at[0, 0], held.at[0, 0], own_sem.at[0]).wait()
-    pl.semaphore_wait(barrier, len(peers))
-
-    def z_copy(q, c):
-        return remote(sent.at[q], band(q, c * rows, rows), z_send.at[0], z_recv.at[q], antipode)
-
-    def y_copy(q, d, c, send):
-        block = band(q, c * rows, rows)
-        return remote(block, block, send.at[d], y_recv.at[d, q], {"y": (up, down)[d]})
-
-    def op_copy(q, source):
-        block = band(q, source * 2 * rows, 2 * rows)
-        to = {"y": jnp.where(lax.rem(q, 2) == 0, up, down)}
-        return remote(block, block, op_send.at[0], op_recv.at[q], to)
-
-    def d_copy(q, source, count):
-        block = band(q, source * 2 * rows, 2 * rows * count)
-        return remote(block, block, d_send.at[0], d_recv.at[q], partner)
-
-    def tz_copy(c):
-        return remote(tiles.at[c], tiles.at[c], tz_sem.at[0], tz_sem.at[1], antipode)
-
-    def ty_copy(j, source):
-        block = tiles.at[pl.ds(source * 2, 2)]
-        return remote(block, block, ty_send.at[j], ty_recv.at[4 - j], {"y": lax.rem(y + j, 4)})
-
-    def pair_copy(side):
-        return remote(pairs.at[side], pairs.at[side], p_sem.at[0], p_sem.at[1], antipode)
-
-    def label_send(core):
-        return remote(labs.at[core], labs.at[core], l_sem.at[1], l_sem.at[2], partner)
-
-    tz_copy(cls).start()
-    pair_copy(h).start()
-    for q in range(STEPS):
-        z_copy(q, cls).start()
-        for d in range(2):
-            y_copy(q, d, cls, yo_send).start()
-    label_send(k).start()
     tz_copy(y * 2 + 1 - h).wait_recv()
     for j in range(1, 4):
         ty_copy(j, y).start()
@@ -191,28 +194,30 @@
         scores = jnp.concatenate(both, axis=1)
         exponent = jnp.exp(scores - jnp.max(scores, axis=0, keepdims=True))
         probs = exponent / jnp.sum(exponent, axis=0, keepdims=True)
-        turn = lax.rem(q, 2)
-        factors[turn] = pair_weights(pairs[k], probs)
+        later_factors[...] = pair_weights(pairs[k], probs)
         lab_rows = [
             labs[core, pl.ds(q * (half // 128) + i, 1), :] for core in range(2) for i in range(half // 128)
         ]
         lab = jnp.concatenate(lab_rows, axis=1)
         one_hot = lax.broadcasted_iota(jnp.int32, (8, 2 * half), 0) == lab
-        resids[turn] = jnp.where(one_hot, 1.0, 0.0) - probs
+        later_resids[...] = jnp.where(one_hot, 1.0, 0.0) - probs
+
+    def next_chunk():
+        factors[...] = later_factors[...]
+        resids[...] = later_resids[...]
 
     def add_products(q, s):
-        turn = lax.rem(q, 2)
         left, right, extra = None, None, None
         for core in range(2):
             block = held[q, core]
             span = slice(core * half, (core + 1) * half)
-            scaled = (block.astype(F32) * factors[turn, s : s + 1, span]).astype(BF16)
+            scaled = (block.astype(F32) * factors[s : s + 1, span]).astype(BF16)
             first = lax.dot_general(scaled[:256], block[:256], contract, preferred_element_type=F32)
             second = lax.dot_general(scaled, block[256:], contract, preferred_element_type=F32)
             left = first if left is None else left + first
             right = second if right is None else right + second
             if s == 0:
-                resid = resids[turn, :, span].astype(BF16)
+                resid = resids[:, span].astype(BF16)
                 term = lax.dot_general(resid, block, contract, preferred_element_type=F32)
                 extra = term if extra is None else extra + term
         total[s, 0:2, :, :, 0:256] += left.reshape(2, 4, 32, 256)
@@ -235,6 +240,7 @@
         matrix[c : c + 1, :] = jnp.concatenate([tile[j : j + 1, :] for j in range(4)], axis=1)
     wait_partner(0)
     prepare(0)
+    next_chunk()
 
     def step(t, carry):
         for stage, first in ((stage_a, 6), (stage_b, 4), (stage_c, 2)):
@@ -244,10 +250,10 @@
                 stage(t + first)
 
         wait_partner(t + 1)
+        prepare(t + 1)
         for s in range(5):
             add_products(t, s)
-            if s == 0:
-                prepare(t + 1)
+        next_chunk()
         return carry
 
     lax.fori_loop(0, STEPS - 1, step, 0)
@@ -263,14 +269,17 @@
         tile = scales.at[source, s]
         return remote(tile, tile, s_send.at[0], s_recv.at[4 - j, s], {"x": around(j)})
 
-    def relay_copy(s):
-        return remote(relay_q.at[s], got_relay.at[s], q_send.at[0], relay_recv.at[s], {"x": around(turn(s)[0])})
-
-    def direct_copy(s):
-        return remote(direct_q.at[s], got_direct.at[s], q_send.at[1], direct_recv.at[s], {"x": around(turn(s)[1])})
-
-    def joint_copy(s):
-        return remote(joint_q.at[s], got_joint.at[s], q_send.at[2], joint_recv.at[s], {"x": around(turn(s)[0])})
+    def relay_copy(s, b):
+        to = {"x": around(turn(s)[0])}
+        return remote(relay_q.at[s, b], got_relay.at[s, b], q_send.at[0], relay_recv.at[s, b], to)
+
+    def direct_copy(s, b):
+        to = {"x": around(turn(s)[1])}
+        return remote(direct_q.at[s, b], got_direct.at[s, b], q_send.at[1], direct_recv.at[s, b], to)
+
+    def joint_copy(s, b):
+        to = {"x": around(turn(s)[0])}
+        return remote(joint_q.at[s, b], got_joint.at[s, b], q_send.at[2], joint_recv.at[s, b], to)
 
     def g_copy(j, source):
         return remote(grads.at[source], grads.at[source], g_send.at[0], g_recv.at[4 - j], {"x": around(j)})
@@ -279,8 +288,8 @@
         top = jnp.max(jnp.max(jnp.abs(block), axis=0, keepdims=True), axis=1, keepdims=True)
         return jnp.maximum(top, 1e-30)
 
-    def piece(s, j):
-        return total[s, :, pl.ds(around(j), 1)].reshape(128, 512)
+    def piece(s, j, b):
+        return total[s, 2 * b : 2 * b + 2, pl.ds(around(j), 1)].reshape(64, 512)
 
     def code(block, inverse):
         return jnp.round(block * inverse).astype(jnp.int32).astype(jnp.int16)
@@ -301,32 +310,44 @@
         top = largest_of(total[s].reshape(512, 512))
         scales[x, s] = jnp.broadcast_to(top * (1.0 / LEVELS), (8, 128))
         inverse = LEVELS / top
-        relay_q[s] = code(piece(s, 2), inverse)
-        for j in (1, 3, 2):
-            s_copy(s, j, x).start()
-        relay_copy(s).start()
-        direct_q[s] = code(piece(s, turn(s)[1]), inverse)
-        direct_copy(s).start()
+        for b in range(2):
+            relay_q[s, b] = code(piece(s, 2, b), inverse)
+            if b == 0:
+                for j in (1, 3, 2):
+                    s_copy(s, j, x).start()
+            relay_copy(s, b).start()
+        for b in range(2):
+            direct_q[s, b] = code(piece(s, turn(s)[1], b), inverse)
+            direct_copy(s, b).start()
 
     def s_wait(s, j):
         tile = scales.at[around(j), s]
         remote(tile, tile, s_send.at[0], s_recv.at[j, s], {"x": around(j)}).wait_recv()
 
-    def joint_sums(s):
+    def joint_sums(s, b):
         ahead, behind = turn(s)
-        relay_copy(s).wait_recv()
-        s_wait(s, behind)
+        relay_copy(s, b).wait_recv()
+        if b == 0:
+            s_wait(s, behind)
         scale, own = scale_of(behind, s), scale_of(0, s)
-        value = plain(got_relay[s]) * scale + piece(s, ahead)
-        joint_q[s] = code(value, 1.0 / (scale + own))
-        joint_copy(s).start()
+        value = plain(got_relay[s, b]) * scale + piece(s, ahead, b)
+        joint_q[s, b] = code(value, 1.0 / (scale + own))
+        joint_copy(s, b).start()
 
     def owner(i, e):
         return {"zl": lax.rem(zl + i, 4), "zh": k, "core": lax.rem(k + e, 2)}
 
-    def f_copy(s, i, e):
-        src = coded.at[s, lax.rem(zl + i, 4), lax.rem(k + e, 2)]
-        return remote(src, far.at[s, z], f_send.at[i, e], f_recv.at[s], owner(i, e))
+    def f_copy(s, block, e):
+        to = {"zl": block, "zh": k, "core": lax.rem(k + e, 2)}
+        return remote(coded.at[s, block, lax.rem(k + e, 2)], far.at[s, z], f_send.at[block, e], f_recv.at[s], to)
+
+    def to_blocks(blocks, act):
+        for block in blocks:
+            for e in range(2):
+                if e:
+                    act(block, e)
+                else:
+                    pl.when((h != k) | (zl != block))(lambda: act(block, 0))
 
     def fs_copy(i, e):
         src = small.at[lax.rem(zl + i, 4)]
@@ -340,67 +361,74 @@
                 else:
                     pl.when(h != k)(lambda: act(0, 0))
 
-    def last_sums(s):
+    def last_sums(s, b):
         ahead, behind = turn(s)
-        joint_copy(s).wait_recv()
-        direct_copy(s).wait_recv()
-        s_wait(s, ahead)
-        s_wait(s, 2)
-        value = piece(s, 0) + plain(got_direct[s]) * scale_of(ahead, s)
-        value += plain(got_joint[s]) * (scale_of(behind, s) + scale_of(2, s))
+        joint_copy(s, b).wait_recv()
+        direct_copy(s, b).wait_recv()
+        if b == 0:
+            s_wait(s, ahead)
+            s_wait(s, 2)
+        value = piece(s, 0, b) + plain(got_direct[s, b]) * scale_of(ahead, s)
+        value += plain(got_joint[s, b]) * (scale_of(behind, s) + scale_of(2, s))
         top = largest_of(value)
         out = code(value, LEVELS / top)
-        for i in range(4):
+        for i in range(2):
             for e in range(2):
                 first = i * 32 + e * 16
-                coded[s, i, e] = out[first : first + 16, :]
-        to_owners(lambda i, e: f_copy(s, i, e).start())
-        pl.when(h == k)(lambda: pltpu.make_async_copy(coded.at[s, zl, k], far.at[s, z], f_recv.at[s]).start())
+                coded[s, 2 * b + i, e] = out[first : first + 16, :]
+        to_blocks((2 * b, 2 * b + 1), lambda block, e: f_copy(s, block, e).start())
+
+        @pl.when((h == k) & (zl // 2 == b))
+        def _():
+            pltpu.make_async_copy(coded.at[s, zl, k], far.at[s, z], f_recv.at[s]).start()
+
         return top * (1.0 / LEVELS)
 
-    def b_copy(i, e):
-        src = b_q.at[lax.rem(zl + i, 4), lax.rem(k + e, 2)]
-        return remote(src, far_b.at[z], b_send.at[i, e], b_recv.at[0], owner(i, e))
-
-    def bs_copy(i, e):
-        return remote(b_scale, far_bs.at[z], bs_send.at[i, e], bs_recv.at[0], owner(i, e))
-
-    def bx_copy(j, source):
-        return remote(b_sum.at[around(j)], got_b.at[source], bx_send.at[0], bx_recv.at[4 - j], {"x": around(j)})
-
-    def beta_sums(s):
+    def b_copy(n, i, e):
+        src = b_q.at[n, lax.rem(zl + i, 4), lax.rem(k + e, 2)]
+        return remote(src, far_b.at[n, z], b_send.at[n, i, e], b_recv.at[n], owner(i, e))
+
+    def bs_copy(n, i, e):
+        return remote(b_scale.at[n], far_bs.at[n, z], bs_send.at[n, i, e], bs_recv.at[n], owner(i, e))
+
+    def bx_copy(n, j, source):
+        src = b_sum.at[n, around(j)]
+        return remote(src, got_b.at[n, source], bx_send.at[n], bx_recv.at[n, 4 - j], {"x": around(j)})
+
+    def beta_sums(n):
+        s = AROUND + n
         finish(s)
         top = largest_of(total[s].reshape(512, 512))
-        b_scale[...] = jnp.broadcast_to(top * (1.0 / LEVELS), (8, 128))
+        b_scale[n] = jnp.broadcast_to(top * (1.0 / LEVELS), (8, 128))
         inverse = LEVELS / top
         for i in range(4):
             for c in range(2):
                 for p in range(4):
-                    b_q[i, c, 16 * p : 16 * (p + 1), :] = code(total[s, i, p, 16 * c : 16 * (c + 1), :], inverse)
-        to_owners(lambda i, e: b_copy(i, e).start())
-        to_owners(lambda i, e: bs_copy(i, e).start())
+                    b_q[n, i, c, 16 * p : 16 * (p + 1), :] = code(total[s, i, p, 16 * c : 16 * (c + 1), :], inverse)
+        to_owners(lambda i, e: b_copy(n, i, e).start())
+        to_owners(lambda i, e: bs_copy(n, i, e).start())
 
         @pl.when(h == k)
         def _():
-            pltpu.make_async_copy(b_q.at[zl, k], far_b.at[z], b_recv.at[0]).start()
-            pltpu.make_async_copy(b_scale, far_bs.at[z], bs_recv.at[0]).start()
-
-    def cross_sums():
-        pltpu.make_async_copy(far_b, far_b, b_recv.at[0]).wait()
-        pltpu.make_async_copy(far_bs, far_bs, bs_recv.at[0]).wait()
+            pltpu.make_async_copy(b_q.at[n, zl, k], far_b.at[n, z], b_recv.at[n]).start()
+            pltpu.make_async_copy(b_scale.at[n], far_bs.at[n, z], bs_recv.at[n]).start()
+
+    def cross_sums(n):
+        pltpu.make_async_copy(far_b.at[n], far_b.at[n], b_recv.at[n]).wait()
+        pltpu.make_async_copy(far_bs.at[n], far_bs.at[n], bs_recv.at[n]).wait()
         value = jnp.zeros((64, 512), F32)
         for source in range(8):
-            value += plain(far_b[source]) * far_bs[source, 0:1, 0:1]
-        b_sum[...] = value.reshape(4, 16, 512)
+            value += plain(far_b[n, source]) * far_bs[n, source, 0:1, 0:1]
+        b_sum[n] = value.reshape(4, 16, 512)
         for j in (1, 3, 2):
-            bx_copy(j, x).start()
+            bx_copy(n, j, x).start()
 
     scale2 = jnp.zeros((8, 128), F32)
-    for act, s in ORDER:
+    for act, s, b in ORDER:
         if act == "beta":
-            beta_sums(s)
+            beta_sums(s - AROUND)
         if act == "cross":
-            cross_sums()
+            cross_sums(s - AROUND)
         if act == "first":
             first_sums(s)
             if s == 0:
@@ -408,9 +436,9 @@
                 for j in (1, 3, 2):
                     g_copy(j, x).start()
         if act == "joint":
-            joint_sums(s)
+            joint_sums(s, b)
         if act == "last":
-            scale2 = jnp.where(row8 == s, last_sums(s), scale2)
+            scale2 = jnp.where(row8 == 2 * s + b, last_sums(s, b), scale2)
 
     for j in (1, 3, 2):
         g_copy(4 - j, around(4 - j)).wait_recv()
@@ -441,16 +469,17 @@
     stage[...] = pltpu.roll(final, lax.rem(128 - (x * 32 + k * 16), 128), 1)
     grad_out[...] = stage[0:1, 0:16]
     for s in range(5):
-        if s == 4:
-            value = b_sum[x]
+        if s >= AROUND:
+            n = s - AROUND
+            value = b_sum[n, x]
             for j in (1, 3, 2):
-                bx_copy(4 - j, around(j)).wait_recv()
-                value += got_b[around(j)]
+                bx_copy(n, 4 - j, around(j)).wait_recv()
+                value += got_b[n, around(j)]
         else:
             pltpu.make_async_copy(far.at[s], far.at[s], f_recv.at[s]).wait()
             value = jnp.zeros((16, 512), F32)
             for source in range(8):
-                value += plain(far[s, source]) * far_small[source, 1, s : s + 1, 0:1]
+                value += plain(far[s, source]) * far_small[source, 1, pl.ds(2 * s + zl // 2, 1), 0:1]
         smooth = jnp.float32(0.0)
         for j, number in enumerate(DIAGONAL):
             smooth += jnp.where(slots[s] == number, smoothing[j], 0.0)
@@ -471,13 +500,14 @@
     sent_all(held.at[0], op_send.at[0])
     sent_all(held.at[pl.ds(0, STEPS // 2)], d_send.at[0])
     sent_all(scales.at[pl.ds(0, 3)], s_send.at[0])
-    sent_all(got_b.at[pl.ds(0, 3)], bx_send.at[0])
-    to_owners(lambda i, e: b_copy(i, e).wait_send())
-    to_owners(lambda i, e: bs_copy(i, e).wait_send())
+    for n in range(5 - AROUND):
+        sent_all(got_b.at[n, pl.ds(0, 3)], bx_send.at[n])
+        to_owners(lambda i, e: b_copy(n, i, e).wait_send())
+        to_owners(lambda i, e: bs_copy(n, i, e).wait_send())
     for i in range(3):
         sent_all(relay_q, q_send.at[i])
     sent_all(grads.at[pl.ds(0, 3)], g_send.at[0])
-    to_owners(lambda i, e: sent_all(coded.at[:, 0, 0], f_send.at[i, e]))
+    to_blocks(range(4), lambda block, e: sent_all(coded.at[:, 0, 0], f_send.at[block, e]))
     to_owners(lambda i, e: fs_copy(i, e).wait_send())
 
 
@@ -487,12 +517,14 @@
     anyspace = pl.BlockSpec(memory_space=pl.ANY)
     dma = pltpu.SemaphoreType.DMA
     half = features.shape[1] // 2 // STEPS
-    block = pltpu.VMEM((4, 128, 512), jnp.int16)
+    late = 5 - AROUND
+    wide = pltpu.VMEM((8, 2 * half), F32)
+    block = pltpu.VMEM((AROUND, 2, 64, 512), jnp.int16)
     hessian, gradient = pl.pallas_call(
         newton_kernel,
         out_shape=(
-            jax.ShapeDtypeStruct((5, 16, 512), F32),
-            jax.ShapeDtypeStruct((1, 16), F32),
+            pltpu.VMEM((5, 16, 512), F32),
+            pltpu.VMEM((1, 16), F32),
         ),
         in_specs=[anyspace, vmem, anyspace, smem, smem],
         out_specs=(vmem, vmem),
@@ -504,30 +536,29 @@
             pltpu.VMEM((2, 8, 128), jnp.int32),
             pltpu.VMEM((8, 8, 128), F32),
             pltpu.VMEM((8, 512), F32),
-            pltpu.VMEM((2, 8, 2 * half), F32),
-            pltpu.VMEM((2, 8, 2 * half), F32),
+            wide, wide, wide, wide,
             pltpu.VMEM((8, 512), F32),
-            pltpu.VMEM((4, 4, 8, 128), F32),
+            pltpu.VMEM((4, AROUND, 8, 128), F32),
             block, block, block, block, block, block,
             pltpu.VMEM((4, 8, 512), F32),
-            pltpu.VMEM((4, 4, 2, 16, 512), jnp.int16),
+            pltpu.VMEM((AROUND, 4, 2, 16, 512), jnp.int16),
             pltpu.VMEM((4, 2, 8, 128), F32),
-            pltpu.VMEM((4, 8, 16, 512), jnp.int16),
+            pltpu.VMEM((AROUND, 8, 16, 512), jnp.int16),
             pltpu.VMEM((8, 2, 8, 128), F32),
-            pltpu.VMEM((4, 2, 64, 512), jnp.int16),
-            pltpu.VMEM((8, 128), F32),
-            pltpu.VMEM((8, 64, 512), jnp.int16),
-            pltpu.VMEM((8, 8, 128), F32),
-            pltpu.VMEM((4, 16, 512), F32),
-            pltpu.VMEM((4, 16, 512), F32),
+            pltpu.VMEM((late, 4, 2, 64, 512), jnp.int16),
+            pltpu.VMEM((late, 8, 128), F32),
+            pltpu.VMEM((late, 8, 64, 512), jnp.int16),
+            pltpu.VMEM((late, 8, 8, 128), F32),
+            pltpu.VMEM((late, 4, 16, 512), F32),
+            pltpu.VMEM((late, 4, 16, 512), F32),
             pltpu.VMEM((8, 512), F32),
             pltpu.VMEM((8, 128), F32),
             dma((1,)), dma((1,)), dma((1,)), dma((STEPS,)), dma((2,)), dma((2,)), dma((2, STEPS)),
             dma((1,)), dma((STEPS,)), dma((1,)), dma((STEPS,)),
             dma((2,)), dma((4,)), dma((4,)), dma((2,)), dma((3,)),
-            dma((1,)), dma((4, 4)), dma((3,)), dma((4,)), dma((4,)), dma((4,)),
-            dma((1,)), dma((4,)), dma((4, 2)), dma((4,)), dma((4, 2)), dma((1,)),
-            dma((4, 2)), dma((1,)), dma((4, 2)), dma((1,)), dma((1,)), dma((4,)),
+            dma((1,)), dma((4, AROUND)), dma((3,)), dma((AROUND, 2)), dma((AROUND, 2)), dma((AROUND, 2)),
+            dma((1,)), dma((4,)), dma((4, 2)), dma((AROUND,)), dma((4, 2)), dma((1,)),
+            dma((late, 4, 2)), dma((late,)), dma((late, 4, 2)), dma((late,)), dma((late,)), dma((late, 4)),
         ],
         compiler_params=pltpu.CompilerParams(collective_id=0, has_side_effects=True),
         name="newton",

time: 78.6 us -> 74.7 us (0.950)
  Pallas kernels: 75.6 us -> 72.8 us
  local copies, waits for them, and re-layouts: 2.11 us -> 1.18 us
    pallas_call x1, Pallas kernels: 75.6 us -> 72.8 us  [local(): pl.pallas_call(newton_kernel, out_shape=(pltpu.VMEM((5, 16, 512), F32), p...]
    unnamed x4 -> x2, local copies, waits for them, and re-layouts: 2.11 us -> 1.18 us
where the time goes in v4:
time: 74.7 us; the launch traced here: 74.6 us
  Pallas kernels  72.8 us (97%)
  local copies, waits for them, and re-layouts  1.18 us (2%)
    pallas_call x1, Pallas kernels, local(): pl.pallas_call(newton_kernel, out_shape=(pltpu.VMEM((5, 16, 512), F32), p...  72.8 us

profile of v4, /device:TPU:1, one launch (start us, length us, event | category | flops | bytes accessed | tf_op | source)
XLA Modules:
  0.0 74.6 jit_solution(5576557181898559002)
XLA Ops:
  0.6 72.8 %newton.1 = (f32[5,16,512]{2,1,0:T(8,128)S(1)}, f32[1,16]{1,0:T(1,128)S(1)}) custom-call(bf16[64,4096]{1,0:T(8,128)(2,1)} %feat.1, bf16[1,512]{1,0:T(2,128)(2,1)} %coeffs.1, s32[32,128]{1,0:T(8,128)} %bitcast.3, s32[5]{0:T(128)} %slots.1, f32[8]{0:T(128)} %smoothing.1), custom_call_target="tpu_custom_call" | custom-call | tf_op jit(solution)/shard_map/newton/pallas_call | solution.py:523
  73.4 0.7 copy.9
  74.1 0.5 copy.10

commit v5 on v4

--- a/solution.py
+++ b/solution.py
@@ -19,8 +19,8 @@
 LEVELS = 32767.0
 ORDER = (
     ("first", 0, 0), ("first", 1, 0), ("beta", 4, 0), ("joint", 0, 0), ("joint", 0, 1), ("first", 2, 0), ("joint", 1, 0), ("joint", 1, 1), ("first", 3, 0),
-    ("last", 0, 0), ("joint", 2, 0), ("last", 0, 1), ("joint", 2, 1), ("last", 1, 0), ("joint", 3, 0), ("last", 1, 1), ("joint", 3, 1),
-    ("last", 2, 0), ("last", 2, 1), ("cross", 4, 0), ("last", 3, 0), ("last", 3, 1),
+    ("last", 0, 0), ("joint", 2, 0), ("last", 0, 1), ("joint", 2, 1), ("last", 1, 0), ("last", 1, 1), ("joint", 3, 0), ("last", 2, 0), ("joint", 3, 1), ("last", 2, 1),
+    ("cross", 4, 0), ("last", 3, 0), ("last", 3, 1),
 )
 F32 = jnp.float32
 BF16 = jnp.bfloat16
@@ -292,7 +292,7 @@
         return total[s, 2 * b : 2 * b + 2, pl.ds(around(j), 1)].reshape(64, 512)
 
     def code(block, inverse):
-        return jnp.round(block * inverse).astype(jnp.int32).astype(jnp.int16)
+        return jnp.floor(block * inverse + 0.5).astype(jnp.int32).astype(jnp.int16)
 
     def plain(block):
         return block.astype(jnp.int32).astype(F32)
@@ -370,7 +370,7 @@
             s_wait(s, 2)
         value = piece(s, 0, b) + plain(got_direct[s, b]) * scale_of(ahead, s)
         value += plain(got_joint[s, b]) * (scale_of(behind, s) + scale_of(2, s))
-        top = largest_of(value)
+        top = (scale_of(0, s) + scale_of(1, s) + scale_of(2, s) + scale_of(3, s)) * LEVELS
         out = code(value, LEVELS / top)
         for i in range(2):
             for e in range(2):

time: 74.7 us -> 74.4 us (level)
  no operation moved by 1% of the time
where the time goes in v5:
time: 74.4 us; the launch traced here: 74.3 us
  Pallas kernels  72.5 us (97%)
  local copies, waits for them, and re-layouts  1.18 us (2%)
    pallas_call x1, Pallas kernels, local(): pl.pallas_call(newton_kernel, out_shape=(pltpu.VMEM((5, 16, 512), F32), p...  72.5 us

profile of v5, /device:TPU:1, one launch (start us, length us, event | category | flops | bytes accessed | tf_op | source)
XLA Modules:
  0.0 74.3 jit_solution(10916240457534751223)
XLA Ops:
  0.6 72.5 %newton.1 = (f32[5,16,512]{2,1,0:T(8,128)S(1)}, f32[1,16]{1,0:T(1,128)S(1)}) custom-call(bf16[64,4096]{1,0:T(8,128)(2,1)} %feat.1, bf16[1,512]{1,0:T(2,128)(2,1)} %coeffs.1, s32[32,128]{1,0:T(8,128)} %bitcast.3, s32[5]{0:T(128)} %slots.1, f32[8]{0:T(128)} %smoothing.1), custom_call_target="tpu_custom_call" | custom-call | tf_op jit(solution)/shard_map/newton/pallas_call | solution.py:523
  73.2 0.7 copy.9
  73.8 0.5 copy.10
